TPU v7x, 32 devices: a whole 2x2x4 slice. The times are simulated.
32 devices in a mesh: rep: 2 (over x), dp: 16 (over y, z, core).
Axes of the slice: x: 2, y: 2, z: 4, core: 2. Of those that a mesh axis runs over, the one named last changes fastest.
Arguments:
- g_w_gate: bfloat16 [32, 2, 1024, 4096], P(('rep', 'dp')), parts along dimension 0
- g_w_up: bfloat16 [32, 2, 1024, 4096], P(('rep', 'dp')), parts along dimension 0
- g_w_down: bfloat16 [32, 2, 4096, 1024], P(('rep', 'dp')), parts along dimension 0
- w_gate: bfloat16 [2, 1024, 4096], replicated
- w_up: bfloat16 [2, 1024, 4096], replicated
- w_down: bfloat16 [2, 4096, 1024], replicated
- m_w_gate: float32 [2, 1024, 4096], P(None, 'dp')
- m_w_up: float32 [2, 1024, 4096], P(None, 'dp')
- m_w_down: float32 [2, 4096, 1024], P(None, 'dp')
- v_w_gate: float32 [2, 1024, 4096], P(None, 'dp')
- v_w_up: float32 [2, 1024, 4096], P(None, 'dp')
- v_w_down: float32 [2, 4096, 1024], P(None, 'dp')
Outputs:
- output 1: bfloat16 [4, 1024, 4096], P('rep'), parts along dimension 0
- output 2: bfloat16 [4, 1024, 4096], P('rep'), parts along dimension 0
- output 3: bfloat16 [4, 4096, 1024], P('rep'), parts along dimension 0
- output 4: float32 [4, 1024, 4096], P('rep', 'dp'), parts along dimension 0
- output 5: float32 [4, 1024, 4096], P('rep', 'dp'), parts along dimension 0
- output 6: float32 [4, 4096, 1024], P('rep', 'dp'), parts along dimension 0
- output 7: float32 [4, 1024, 4096], P('rep', 'dp'), parts along dimension 0
- output 8: float32 [4, 1024, 4096], P('rep', 'dp'), parts along dimension 0
- output 9: float32 [4, 4096, 1024], P('rep', 'dp'), parts along dimension 0
There are 2 independent parts. A program takes and returns all parts, laid end to end along the dimension named above; an argument that names none is the same for every part.
All inputs are finite; a program needn't handle non-finite values.
Results may differ from a plain program's by a relative error of at most 0.022.
Values are sent between devices in bfloat16 or wider.
A program may use at most 2 GiB of HBM per device.

v0:
```python
import jax
import jax.numpy as jnp
from jax import lax
from jax.sharding import PartitionSpec as P


def adamw(w, m, v, g):
    m = 0.9 * m + 0.1 * g
    v = 0.95 * v + 0.05 * g * g
    step = m * lax.rsqrt(v + 1e-8) + 0.1 * w
    return (w - 0.02 * step).astype(jnp.bfloat16), m, v


def clipped(gradients, sum_of_squares, count):
    factor = jnp.minimum(1.0, 0.5 * lax.rsqrt(sum_of_squares / count + 1e-30))
    return [g * factor for g in gradients]


def solution(mesh):
    def step(*arrays):
        terms, weights, m, v = (arrays[i : i + 3] for i in (0, 3, 6, 9))
        gradients = [lax.psum_scatter(t[0], "dp", scatter_dimension=1, tiled=True).astype(jnp.float32) for t in terms]
        squares = lax.psum(sum(jnp.sum(g * g) for g in gradients), "dp")
        gradients = clipped(gradients, squares, lax.psum(1, "dp") * sum(g.size for g in gradients))
        me = lax.axis_index("dp")
        own = [lax.dynamic_slice_in_dim(w, me * one.shape[1], one.shape[1], 1).astype(jnp.float32) for w, one in zip(weights, m, strict=True)]
        new = [adamw(w, m, v, g) for w, m, v, g in zip(own, m, v, gradients, strict=True)]
        whole = [lax.all_gather(one[0], "dp", axis=1, tiled=True) for one in new]
        return (*whole, *(one[1] for one in new), *(one[2] for one in new))

    all_of, cut = P(None, None, None), P(None, "dp", None)
    return jax.shard_map(
        step,
        mesh=mesh,
        in_specs=(P(("rep", "dp"), None, None, None),) * 3 + (all_of,) * 3 + (cut,) * 6,
        out_specs=(P("rep", None, None),) * 3 + (P("rep", "dp", None),) * 6,
        check_vma=False,
    )
```

profile of v0, /device:TPU:0, one launch (start us, length us, event | category | flops | bytes accessed | tf_op | source)
XLA Modules:
  0.0 1008.5 jit_solution(7077694423830181821)
XLA Ops:
  7.2 0.7 reduce-scatter.4.cloned.1.call-update
  8.0 0.7 reduce-scatter.6.cloned.1.call-update
  8.7 0.7 reduce-scatter.8.cloned.1.call-update
  9.4 0.0 all-gather.8.cloned.1.call-start
  9.5 181.0 %reduce-scatter.4.cloned.1.call-done = bf16[2,64,4096]{2,1,0:T(8,128)(2,1)} async-done(((bf16[2,1024,4096]{2,1,0:T(8,128)(2,1)}), bf16[2,64,4096]{2,1,0:T(8,128)(2,1)}) %reduce-scatter.4.cloned.1.call-update) | async-done | bytes 1048592 | tf_op jit(solution)/shard_map/reduce_scatter | solution.py:22
  190.4 2.4 fusion.9
  192.8 176.9 %reduce-scatter.6.cloned.1.call-done = bf16[2,64,4096]{2,1,0:T(8,128)(2,1)} async-done(((bf16[2,1024,4096]{2,1,0:T(8,128)(2,1)}), bf16[2,64,4096]{2,1,0:T(8,128)(2,1)}) %reduce-scatter.6.cloned.1.call-update) | async-done | bytes 1048592 | tf_op jit(solution)/shard_map/reduce_scatter | solution.py:22
  369.7 2.4 fusion.10
  373.4 175.6 %reduce-scatter.8.cloned.1.call-done = bf16[2,256,1024]{2,1,0:T(8,128)(2,1)} async-done(((bf16[2,4096,1024]{2,1,0:T(8,128)(2,1)}), bf16[2,256,1024]{2,1,0:T(8,128)(2,1)}) %reduce-scatter.8.cloned.1.call-update) | async-done | bytes 1048592 | tf_op jit(solution)/shard_map/reduce_scatter | solution.py:22
  549.0 2.4 fusion.11
  552.0 32.2 %psum.7 = f32[]{:T(128)} all-reduce(f32[]{:T(128)S(6)} %add.65), channel_id=1, replica_groups=mesh['rep'=2,'dp'=16] {'dp'}, use_global_device_ids=true, to_apply=%region_6.0 | all-reduce | flops 1 | bytes 8 | tf_op jit(solution)/shard_map/psum | solution.py:23
  584.9 5.3 fusion.17
  590.3 0.0 all-gather.4.cloned.1.call-start
  590.3 5.6 fusion.8
  595.9 0.0 all-gather.6.cloned.1.call-start
  596.0 5.5 fusion.14
  601.5 111.9 %all-gather.8.cloned.1.call-done = bf16[2,4096,1024]{2,1,0:T(8,128)(2,1)} async-done(((bf16[2,256,1024]{2,1,0:T(8,128)(2,1)}), bf16[2,4096,1024]{2,1,0:T(8,128)(2,1)}) %all-gather.8.cloned.1.call-update) | async-done | bytes 16777232 | tf_op jit(solution)/shard_map/all_gather | solution.py:28
  713.4 127.1 %all-gather.4.cloned.1.call-done = bf16[2,1024,4096]{2,1,0:T(8,128)(2,1)} async-done(((bf16[2,64,4096]{2,1,0:T(8,128)(2,1)}), bf16[2,1024,4096]{2,1,0:T(8,128)(2,1)}) %all-gather.4.cloned.1.call-update) | async-done | bytes 16777232 | tf_op jit(solution)/shard_map/all_gather | solution.py:28
  840.5 127.1 %all-gather.6.cloned.1.call-done = bf16[2,1024,4096]{2,1,0:T(8,128)(2,1)} async-done(((bf16[2,64,4096]{2,1,0:T(8,128)(2,1)}), bf16[2,1024,4096]{2,1,0:T(8,128)(2,1)}) %all-gather.6.cloned.1.call-update) | async-done | bytes 16777232 | tf_op jit(solution)/shard_map/all_gather | solution.py:28
  967.6 16.8 %copy.24 = bf16[2,1024,4096]{2,1,0:T(8,128)(2,1)} copy(bf16[2,1024,4096]{2,1,0:T(8,128)(2,1)} %all-gather.4.cloned.1.call-done) | data formatting | bytes 33554432
  984.4 8.5 copy.25
  992.9 1.2 slice-done.2
  994.1 1.4 slice-done.3
  995.5 6.2 copy.26
  (21 shorter events, 0.2 us)
Async XLA Ops:
  7.2 183.3 %reduce-scatter.4.cloned.1.call-start = ((), (), s32[]{:S(2)}) async-start(), calls=%async_computation.3 | async-start | bytes 17825792 | tf_op jit(solution)/shard_map/reduce_scatter | solution.py:22
  7.9 361.8 %reduce-scatter.6.cloned.1.call-start = ((), (), s32[]{:S(2)}) async-start(), calls=%async_computation.4 | async-start | bytes 17825792 | tf_op jit(solution)/shard_map/reduce_scatter | solution.py:22
  8.7 540.3 %reduce-scatter.8.cloned.1.call-start = ((), (), s32[]{:S(2)}) async-start(), calls=%async_computation.5 | async-start | bytes 17825792 | tf_op jit(solution)/shard_map/reduce_scatter | solution.py:22
  9.4 575.5 %copy-start.3 = (f32[2,256,1024]{2,1,0:T(8,128)S(1)}, f32[2,256,1024]{2,1,0:T(8,128)}, u32[]{:S(2)}) copy-start(f32[2,256,1024]{2,1,0:T(8,128)} %param.23) | copy-start | bytes 6291460
  9.4 704.0 %all-gather.8.cloned.1.call-start = ((), (), s32[]{:S(2)}) async-start(), calls=%async_computation.8 | async-start | bytes 17825792 | tf_op jit(solution)/shard_map/all_gather | solution.py:28
  584.9 5.4 copy-start.2
  590.3 250.2 %all-gather.4.cloned.1.call-start = ((), (), s32[]{:S(2)}) async-start(), calls=%async_computation.6 | async-start | bytes 17825792 | tf_op jit(solution)/shard_map/all_gather | solution.py:28
  590.3 5.7 copy-start.1
  595.9 371.7 %all-gather.6.cloned.1.call-start = ((), (), s32[]{:S(2)}) async-start(), calls=%async_computation.7 | async-start | bytes 17825792 | tf_op jit(solution)/shard_map/all_gather | solution.py:28
  967.6 16.8 %copy-start = (bf16[2,1024,4096]{2,1,0:T(8,128)(2,1)S(1)}, bf16[2,1024,4096]{2,1,0:T(8,128)(2,1)}, u32[]{:S(2)}) copy-start(bf16[2,1024,4096]{2,1,0:T(8,128)(2,1)} %all-gather.6.cloned.1.call-done) | copy-start | bytes 50331652
  967.6 25.3 %slice-start = ((s8[16777216]{0:T(1024)(128)(4,1)}), s8[4194304]{0:T(1024)(128)(4,1)S(1)}, s32[]{:S(2)}) async-start(s8[16777216]{0:T(1024)(128)(4,1)} %bitcast.6), calls=%async_computation.9 | async-start | bytes 8388608
  967.6 25.3 %slice-start.1 = ((s8[16777216]{0:T(1024)(128)(4,1)}), s8[4194304]{0:T(1024)(128)(4,1)S(1)}, s32[]{:S(2)}) async-start(s8[16777216]{0:T(1024)(128)(4,1)} %bitcast.6), calls=%async_computation.10 | async-start | bytes 8388608
  967.6 26.5 %slice-start.2 = ((s8[16777216]{0:T(1024)(128)(4,1)}), s8[4194304]{0:T(1024)(128)(4,1)S(1)}, s32[]{:S(2)}) async-start(s8[16777216]{0:T(1024)(128)(4,1)} %bitcast.6), calls=%async_computation.11 | async-start | bytes 8388608
  984.4 11.1 %slice-start.3 = ((s8[16777216]{0:T(1024)(128)(4,1)}), s8[4194304]{0:T(1024)(128)(4,1)S(1)}, s32[]{:S(2)}) async-start(s8[16777216]{0:T(1024)(128)(4,1)} %bitcast.6), calls=%async_computation.12 | async-start | bytes 8388608
Sparse Core Ops, SparseCore 0:
  12.1 178.2 reduce-scatter.3
  194.5 175.1 reduce-scatter.5
  373.8 175.1 reduce-scatter.7
  590.4 122.9 all-gather.7
  716.1 124.3 all-gather.3
  843.2 124.3 all-gather.5
where the time goes:
time: 1010 us
  waiting for transfers between devices  902 us (89%)
  local copies, waits for them, and re-layouts  34.1 us (3%)
  blocking collectives  32.2 us (3%)
  other arithmetic  23.6 us (2%)
  between operations  16.8 us (2%)
    reduce_scatter x3, waiting for transfers between devices, step(): lax.psum_scatter(t[0], 'dp', scatter_dimension=1, tiled=True)  533 us
    all_gather x3, waiting for transfers between devices, step(): whole = [lax.all_gather(one[0], 'dp', axis=1, tiled=True) for one in new]  366 us
    unnamed x19, local copies, waits for them, and re-layouts  34.1 us
    psum x1, blocking collectives, step(): squares = lax.psum(sum((jnp.sum(g * g) for g in gradients)), 'dp')  32.2 us
  transfers between devices with their start and end apart: 6, of which 6 were waited for; matrix products, arithmetic and copies ran while one was open for 2% of the time, Pallas kernels for 0%

commit v1 on v0

v1 whole, which is shorter than its diff:
```python
import jax
import jax.numpy as jnp
from jax import lax
from jax.experimental import pallas as pl
from jax.experimental.pallas import tpu as pltpu
from jax.sharding import PartitionSpec as P

MESH = pl.DeviceIdType.MESH
F32 = jnp.float32
BF16 = jnp.bfloat16
CHIPS = 8
CHUNKS = [(d, w) for w in range(3) for d in range(2)]


def device_at(q, c):
    y = q // 4
    z = q + y * (7 - 2 * q)
    return y * 8 + z * 2 + c


def tiles(ref, body):
    rows, cols = ref.shape

    def strip(r, carry):
        at = pl.ds(pl.multiple_of(r * 16, 16), 16)
        for k in range(cols // 1024):
            body(at, pl.ds(k * 1024, 1024))
        return carry

    lax.fori_loop(0, rows // 16, strip, 0)


def kernel(*refs):
    g, wt, m, v = (refs[i : i + 3] for i in (0, 3, 6, 9))
    x, gsum = refs[12:15], refs[15:18]
    factor_ref = refs[18]
    (p_gu, p_dn, r_gu, r_dn, o_gu, o_dn, w_gu, w_dn, m_gu, m_dn, v_gu, v_dn, acc, norms) = refs[19:33]
    (p_send, p_recv, r_send, r_recv, o_sem, state_sem, a_send, a_recv, n_send, n_recv, l_sem, g_sem) = refs[33:]

    rep, dp = lax.axis_index("rep"), lax.axis_index("dp")
    y, z, c = dp // 8, (dp // 2) % 4, dp % 2
    q = z + y * (7 - 2 * z)
    nxt = [(rep, device_at((q + 1) % CHIPS, c)), (rep, device_at((q + 7) % CHIPS, c))]
    partner = (rep, dp + 1 - 2 * c)

    def pick(gu, dn, lead, d, w):
        return gu.at[(*lead, d, w)] if w < 2 else dn.at[(*lead, d)]

    def rows_of(array, w, d, dev, lead=()):
        n = 64 if w < 2 else 256
        return array[w].at[(*lead, d, pl.ds(pl.multiple_of(dev * n, n), n), slice(None))]

    def scattered(s, d):
        return (q + 7 - s + CHIPS) % CHIPS if d == 0 else (q + 1 + s) % CHIPS

    def gathered(h, d):
        return (q + CHIPS - h) % CHIPS if d == 0 else (q + h) % CHIPS

    def own_load(s, d, w):
        return pltpu.make_async_copy(
            rows_of(g, w, d, device_at(scattered(s, d), c), (0,)), pick(o_gu, o_dn, (s % 2,), d, w), o_sem.at[s % 2, d * 3 + w]
        )

    def to_partner(s, d, w):
        return pltpu.make_async_remote_copy(
            rows_of(g, w, d, device_at(scattered(s, d), 1 - c), (0,)),
            pick(p_gu, p_dn, (s,), d, w),
            p_send.at[s, d * 3 + w],
            p_recv.at[s, d * 3 + w],
            device_id=partner,
            device_id_type=MESH,
        )

    def hop(s, d, w):
        return pltpu.make_async_remote_copy(
            pick(p_gu, p_dn, (s,), d, w),
            pick(r_gu, r_dn, (s % 3,), d, w),
            r_send.at[s % 3, d * 3 + w],
            r_recv.at[s % 3, d * 3 + w],
            device_id=nxt[d],
            device_id_type=MESH,
        )

    def state_loads(d, w):
        i = d * 3 + w
        return [
            pltpu.make_async_copy(m[w].at[d], pick(m_gu, m_dn, (), d, w), state_sem.at[0, i]),
            pltpu.make_async_copy(v[w].at[d], pick(v_gu, v_dn, (), d, w), state_sem.at[1, i]),
            pltpu.make_async_copy(rows_of(wt, w, d, dp), pick(w_gu, w_dn, (), d, w), state_sem.at[2, i]),
        ]

    barrier = pltpu.get_barrier_semaphore()
    for dev in (*nxt, partner):
        pl.semaphore_signal(barrier, inc=1, device_id=dev, device_id_type=MESH)
    for d, w in CHUNKS:
        own_load(0, d, w).start()
    pl.semaphore_wait(barrier, 3)
    for s in (0, 1):
        for d, w in CHUNKS:
            to_partner(s, d, w).start()

    def scatter_step(s, first, last):
        if not last:
            for d, w in CHUNKS:
                own_load(s + 1, d, w).start()
            if first:
                for d, w in CHUNKS:
                    to_partner(s + 2, d, w).start()
            else:

                @pl.when(s < 6)
                def _():
                    for d, w in CHUNKS:
                        to_partner(s + 2, d, w).start()

        for d, w in CHUNKS:
            own, theirs = pick(o_gu, o_dn, (s % 2,), d, w), pick(p_gu, p_dn, (s,), d, w)
            own_load(s, d, w).wait()
            to_partner(s, d, w).wait()
            if first:

                def add(rows, cols):
                    theirs[rows, cols] = (own[rows, cols].astype(F32) + theirs[rows, cols].astype(F32)).astype(BF16)

            else:
                before = (s + 2) % 3
                so_far = pick(r_gu, r_dn, (before,), d, w)
                hop(s - 1, d, w).wait_recv()

                def add(rows, cols):
                    total = (own[rows, cols].astype(F32) + theirs[rows, cols].astype(F32)) + so_far[rows, cols].astype(F32)
                    total = total.astype(BF16)
                    theirs[rows, cols] = total
                    if last:
                        acc[...] += total.astype(F32) * total.astype(F32)

            tiles(theirs, add)
            if last:
                pltpu.make_async_copy(theirs, gsum[w].at[d], g_sem.at[d * 3 + w]).start()
            else:
                if not first:

                    @pl.when(s >= 3)
                    def _():
                        hop(s - 3, d, w).wait_send()

                hop(s, d, w).start()

    scatter_step(0, True, False)
    for d, w in CHUNKS:
        for copy in state_loads(d, w):
            copy.start()
    acc[...] = jnp.zeros_like(acc)
    lax.fori_loop(1, 7, lambda s, carry: (scatter_step(s, False, False), carry)[1], 0)
    scatter_step(7, False, True)

    mine = acc[0:8, 0:128] + acc[8:16, 0:128]
    for k in range(1, 8):
        at = pl.ds(k * 128, 128)
        mine += acc[0:8, at] + acc[8:16, at]
    norms[dp] = mine

    def norm_to(r):
        return pltpu.make_async_remote_copy(
            norms.at[dp], norms.at[dp], n_send.at[r], n_recv.at[dp], device_id=(rep, (dp + r) % 16), device_id_type=MESH
        )

    def norm_from(r):
        src = (dp + 16 - r) % 16
        return pltpu.make_async_remote_copy(
            norms.at[src], norms.at[src], n_send.at[r], n_recv.at[src], device_id=(rep, src), device_id_type=MESH
        )

    for r in range(1, 16):
        norm_to(r).start()
    for s in (4, 5, 6):
        for d, w in CHUNKS:
            hop(s, d, w).wait_send()
    for d, w in CHUNKS:
        for copy in state_loads(d, w):
            copy.wait()
    for r in range(1, 16):
        norm_from(r).wait_recv()
    squares = norms[0]
    for k in range(1, 16):
        squares += norms[k]
    count = 16 * 2 * (64 * 4096 * 2 + 256 * 1024)
    mean = jnp.sum(squares) * (1.0 / count)
    factor = jnp.minimum(1.0, 0.5 * lax.rsqrt(jnp.full((8, 128), mean, F32) + 1e-30))
    factor_ref[...] = factor
    scale = jnp.broadcast_to(factor[0:1, 0:1], (16, 1024))

    def gather_hop(h, d, w):
        block = device_at(gathered(h, d), c)
        src = pick(p_gu, p_dn, (0,), d, w) if isinstance(h, int) and h == 0 else rows_of(x, w, d, block)
        return pltpu.make_async_remote_copy(
            src, rows_of(x, w, d, block), a_send.at[h, d * 3 + w], a_recv.at[h, d * 3 + w], device_id=nxt[d], device_id_type=MESH
        )

    def gather_from(h, d, w):
        block = rows_of(x, w, d, device_at(gathered(h, d), c))
        return pltpu.make_async_remote_copy(
            block, block, a_send.at[h - 1, d * 3 + w], a_recv.at[h - 1, d * 3 + w], device_id=nxt[d], device_id_type=MESH
        )

    def share(h, d, w):
        block = device_at(gathered(h, d), c)
        src = pick(p_gu, p_dn, (0,), d, w) if isinstance(h, int) and h == 0 else rows_of(x, w, d, block)
        return pltpu.make_async_remote_copy(
            src, rows_of(x, w, d, block), p_send.at[h, d * 3 + w], p_recv.at[h, d * 3 + w], device_id=partner, device_id_type=MESH
        )

    def shared(h, d, w):
        block = rows_of(x, w, d, device_at(gathered(h, d), 1 - c))
        return pltpu.make_async_remote_copy(
            block, block, p_send.at[h, d * 3 + w], p_recv.at[h, d * 3 + w], device_id=partner, device_id_type=MESH
        )

    def keep(d, w):
        return pltpu.make_async_copy(pick(p_gu, p_dn, (0,), d, w), rows_of(x, w, d, dp), l_sem.at[d * 3 + w])

    for d, w in CHUNKS:
        gr, new = pick(p_gu, p_dn, (7,), d, w), pick(p_gu, p_dn, (0,), d, w)
        mr, vr, wr = pick(m_gu, m_dn, (), d, w), pick(v_gu, v_dn, (), d, w), pick(w_gu, w_dn, (), d, w)

        def update(rows, cols):
            grad = gr[rows, cols].astype(F32) * scale
            m1 = 0.9 * mr[rows, cols] + 0.1 * grad
            v1 = 0.95 * vr[rows, cols] + 0.05 * grad * grad
            old = wr[rows, cols].astype(F32)
            new[rows, cols] = (old - 0.02 * (m1 * lax.rsqrt(v1 + 1e-8) + 0.1 * old)).astype(BF16)

        tiles(new, update)
        gather_hop(0, d, w).start()
        share(0, d, w).start()
        keep(d, w).start()

    def gather_step(h, carry):
        for d, w in CHUNKS:
            gather_from(h, d, w).wait_recv()
            gather_hop(h, d, w).start()
            share(h, d, w).start()
        return carry

    lax.fori_loop(1, 7, gather_step, 0)
    for d, w in CHUNKS:
        gather_from(7, d, w).wait_recv()
        share(7, d, w).start()

    for r in range(1, 16):
        norm_to(r).wait_send()
    for d, w in CHUNKS:
        keep(d, w).wait()
        pltpu.make_async_copy(pick(p_gu, p_dn, (7,), d, w), gsum[w].at[d], g_sem.at[d * 3 + w]).wait()

    def drain(h, carry):
        for d, w in CHUNKS:
            gather_from(h + 1, d, w).wait_send()
        return carry

    lax.fori_loop(0, 7, drain, 0)

    def drain_shares(h, carry):
        for d, w in CHUNKS:
            shared(h, d, w).wait()
        return carry

    lax.fori_loop(0, 8, drain_shares, 0)


def solution(mesh):
    whole = [(2, 1024, 4096), (2, 1024, 4096), (2, 4096, 1024)]
    block = [(2, 64, 4096), (2, 64, 4096), (2, 256, 1024)]

    def pair(lead, dtype):
        return [pltpu.VMEM((*lead, 2, 2, 64, 4096), dtype), pltpu.VMEM((*lead, 2, 256, 1024), dtype)]

    dma = pltpu.SemaphoreType.DMA
    any_space = pl.BlockSpec(memory_space=pl.ANY)

    def step(*arrays):
        out = pl.pallas_call(
            kernel,
            out_shape=[jax.ShapeDtypeStruct(s, BF16) for s in whole + block] + [jax.ShapeDtypeStruct((8, 128), F32)],
            in_specs=[any_space] * 12,
            out_specs=[any_space] * 6 + [pl.BlockSpec(memory_space=pltpu.VMEM)],
            scratch_shapes=[
                *pair((8,), BF16),
                *pair((3,), BF16),
                *pair((2,), BF16),
                *pair((), BF16),
                *pair((), F32),
                *pair((), F32),
                pltpu.VMEM((16, 1024), F32),
                pltpu.VMEM((16, 8, 128), F32),
                dma((8, 6)), dma((8, 6)), dma((3, 6)), dma((3, 6)), dma((2, 6)), dma((3, 6)),
                dma((7, 6)), dma((7, 6)), dma((16,)), dma((16,)), dma((6,)), dma((6,)),
            ],
            compiler_params=pltpu.CompilerParams(collective_id=0, has_side_effects=True, vmem_limit_bytes=66 * 1000 * 1000),
            name="step",
        )(*arrays)
        new_w, sums, factor = out[:3], out[3:6], out[6][0, 0]
        m, v = arrays[6:9], arrays[9:12]
        gs = [s.astype(F32) * factor for s in sums]
        return (*new_w, *(0.9 * a + 0.1 * b for a, b in zip(m, gs)), *(0.95 * a + 0.05 * b * b for a, b in zip(v, gs)))

    all_of, cut = P(None, None, None), P(None, "dp", None)
    return jax.shard_map(
        step,
        mesh=mesh,
        in_specs=(P(("rep", "dp"), None, None, None),) * 3 + (all_of,) * 3 + (cut,) * 6,
        out_specs=(P("rep", None, None),) * 3 + (P("rep", "dp", None),) * 6,
        check_vma=False,
    )
```

time: 1010 us -> 542 us (0.54)
  waiting for transfers between devices: 902 us -> 0 us
  Pallas kernels: 0 us -> 494 us
  blocking collectives: 32.2 us -> 0 us
  between operations: 16.8 us -> 0.73 us
  other arithmetic: 23.6 us -> 13.3 us
    reduce_scatter x3 -> x0, waiting for transfers between devices: 533 us -> none  [step(): lax.psum_scatter(t[0], 'dp', scatter_dimension=1, tiled=True)]
    pallas_call x0 -> x1, Pallas kernels: none -> 494 us  [step(): pl.pallas_call(kernel, out_shape=[jax.ShapeDtypeStruct(s, BF16) for s in...]
    all_gather x3 -> x0, waiting for transfers between devices: 366 us -> none  [step(): whole = [lax.all_gather(one[0], 'dp', axis=1, tiled=True) for one in new]]
    psum x1 -> x0, blocking collectives: 32.2 us -> none  [step(): squares = lax.psum(sum((jnp.sum(g * g) for g in gradients)), 'dp')]
    convert_element_type x3 -> x0, other arithmetic: 16.5 us -> none  [adamw(): return ((w - 0.02 * step).astype(jnp.bfloat16), m, v)]
    add x0 -> x2, other arithmetic: none -> 13.3 us  [step(): 0.95 * a + 0.05 * b * b]
    unnamed x19 -> x25, local copies, waits for them, and re-layouts: 34.1 us -> 32.9 us
  transfers between devices with their start and end apart: 6 -> 0, of which waited for: 6 -> 0; matrix products, arithmetic and copies ran while one was open for 2% -> 0% of each run, Pallas kernels for 0% -> 0%
where the time goes in v1:
time: 542 us
  Pallas kernels  494 us (91%)
  local copies, waits for them, and re-layouts  34.1 us (6%)
  other arithmetic  13.3 us (2%)
    pallas_call x1, Pallas kernels, step(): pl.pallas_call(kernel, out_shape=[jax.ShapeDtypeStruct(s, BF16) for s in...  494 us
    unnamed x25, local copies, waits for them, and re-layouts  32.9 us
    add x2, other arithmetic, step(): 0.95 * a + 0.05 * b * b  13.3 us

profile of v1, /device:TPU:0, one launch (start us, length us, event | category | flops | bytes accessed | tf_op | source)
XLA Modules:
  0.0 541.9 jit_solution(12602562850222924650)
XLA Ops:
  0.6 493.7 %step.1 = (bf16[2,1024,4096]{2,1,0:T(8,128)(2,1)}, bf16[2,1024,4096]{2,1,0:T(8,128)(2,1)}, bf16[2,4096,1024]{2,1,0:T(8,128)(2,1)}, bf16[2,64,4096]{2,1,0:T(8,128...) custom-call(bf16[1,2,1024,4096]{3,2,1,0:T(8,128)(2,1)} %refs_0_.1, ...), custom_call_target="tpu_custom_call" | custom-call | tf_op jit(solution)/shard_map/step/pallas_call | solution.py:282
  494.4 1.2 slice.3
  495.6 0.0 copy-start
  495.6 0.0 copy-start.1
  495.6 9.8 %fusion = (f32[2,64,4096]{2,1,0:T(8,128)}, f32[2,64,4096]{2,1,0:T(8,128)}, f32[2,64,4096]{2,1,0:T(8,128)}, f32[2,64,4096]{2,1,0:T(8,128)}) fusion(f32[2,64,4096]{2,1,0:T(8,128)} %refs_9_.1, bf16[2,64,4096]{2,1,0:T(8,128)(2,1)} %get-tuple-element.19, f32[]{:T(128)} %bitcast, f32[2,64,4096]{2,1,0:T(8,128)} %refs_6_.1, ...), kind=kLoop, calls=%fused_computation.3 | loop fusion | flops 9437184 | bytes 18874372 | tf_op jit(solution)/shard_map/add | solution.py:305
  505.4 0.0 copy-done
  505.4 0.0 copy-done.1
  505.4 0.0 copy-done.2
  505.4 0.0 slice-start.4
  505.4 3.5 fusion.2
  508.9 0.0 slice-start.1
  508.9 16.8 %copy.24 = bf16[2,1024,4096]{2,1,0:T(8,128)(2,1)} copy(bf16[2,1024,4096]{2,1,0:T(8,128)(2,1)} %get-tuple-element.40) | data formatting | bytes 33554432
  525.7 0.0 slice-done.4
  525.7 0.0 slice-done.5
  525.7 0.0 slice-done.6
  525.7 0.0 slice-done.7
  525.8 0.0 slice-start.2
  525.8 0.0 slice-start.3
  525.8 8.5 %copy.25 = bf16[2,1024,4096]{2,1,0:T(8,128)(2,1)} copy(bf16[2,1024,4096]{2,1,0:T(8,128)(2,1)S(1)} %bitcast.4) | data formatting | bytes 33554432
  534.3 0.0 slice-done
  534.3 0.0 slice-done.1
  534.3 0.0 slice-done.2
  534.3 1.4 slice-done.3
  535.7 6.2 %copy.26 = bf16[2,4096,1024]{2,1,0:T(8,128)(2,1)} copy(bf16[2,4096,1024]{2,1,0:T(8,128)(2,1)S(1)} %bitcast.2) | data formatting | bytes 33554432
  (7 shorter events, 0.0 us)
Async XLA Ops:
  495.6 9.8 %copy-start = (f32[2,256,1024]{2,1,0:T(8,128)S(1)}, f32[2,256,1024]{2,1,0:T(8,128)}, u32[]{:S(2)}) copy-start(f32[2,256,1024]{2,1,0:T(8,128)} %refs_8_.1) | copy-start | bytes 6291460
  495.6 9.8 %copy-start.1 = (f32[2,256,1024]{2,1,0:T(8,128)S(1)}, f32[2,256,1024]{2,1,0:T(8,128)}, u32[]{:S(2)}) copy-start(f32[2,256,1024]{2,1,0:T(8,128)} %refs_11_.1) | copy-start | bytes 6291460
  495.6 9.8 %copy-start.2 = (bf16[2,256,1024]{2,1,0:T(8,128)(2,1)S(1)}, bf16[2,256,1024]{2,1,0:T(8,128)(2,1)}, u32[]{:S(2)}) copy-start(bf16[2,256,1024]{2,1,0:T(8,128)(2,1)} %get-tuple-element.22) | copy-start | bytes 3145732
  505.4 20.4 %slice-start.4 = ((s8[16777216]{0:T(1024)(128)(4,1)}), s8[4194304]{0:T(1024)(128)(4,1)S(1)}, s32[]{:S(2)}) async-start(s8[16777216]{0:T(1024)(128)(4,1)} %bitcast.3), calls=%async_computation.4 | async-start | bytes 8388608
  508.9 16.8 %slice-start.5 = ((s8[16777216]{0:T(1024)(128)(4,1)}), s8[4194304]{0:T(1024)(128)(4,1)S(1)}, s32[]{:S(2)}) async-start(s8[16777216]{0:T(1024)(128)(4,1)} %bitcast.3), calls=%async_computation.5 | async-start | bytes 8388608
  508.9 16.8 %slice-start.6 = ((s8[16777216]{0:T(1024)(128)(4,1)}), s8[4194304]{0:T(1024)(128)(4,1)S(1)}, s32[]{:S(2)}) async-start(s8[16777216]{0:T(1024)(128)(4,1)} %bitcast.3), calls=%async_computation.6 | async-start | bytes 8388608
  508.9 16.9 %slice-start.7 = ((s8[16777216]{0:T(1024)(128)(4,1)}), s8[4194304]{0:T(1024)(128)(4,1)S(1)}, s32[]{:S(2)}) async-start(s8[16777216]{0:T(1024)(128)(4,1)} %bitcast.3), calls=%async_computation.7 | async-start | bytes 8388608
  508.9 25.4 %slice-start = ((s8[16777216]{0:T(1024)(128)(4,1)}), s8[4194304]{0:T(1024)(128)(4,1)S(1)}, s32[]{:S(2)}) async-start(s8[16777216]{0:T(1024)(128)(4,1)} %bitcast.1), calls=%async_computation | async-start | bytes 8388608
  508.9 25.4 %slice-start.1 = ((s8[16777216]{0:T(1024)(128)(4,1)}), s8[4194304]{0:T(1024)(128)(4,1)S(1)}, s32[]{:S(2)}) async-start(s8[16777216]{0:T(1024)(128)(4,1)} %bitcast.1), calls=%async_computation.1 | async-start | bytes 8388608
  525.8 8.5 %slice-start.2 = ((s8[16777216]{0:T(1024)(128)(4,1)}), s8[4194304]{0:T(1024)(128)(4,1)S(1)}, s32[]{:S(2)}) async-start(s8[16777216]{0:T(1024)(128)(4,1)} %bitcast.1), calls=%async_computation.2 | async-start | bytes 8388608
  525.8 9.9 %slice-start.3 = ((s8[16777216]{0:T(1024)(128)(4,1)}), s8[4194304]{0:T(1024)(128)(4,1)S(1)}, s32[]{:S(2)}) async-start(s8[16777216]{0:T(1024)(128)(4,1)} %bitcast.1), calls=%async_computation.3 | async-start | bytes 8388608

commit v2 on v1

--- a/solution.py
+++ b/solution.py
@@ -5,10 +5,12 @@
 from jax.experimental.pallas import tpu as pltpu
 from jax.sharding import PartitionSpec as P
 
+
 MESH = pl.DeviceIdType.MESH
 F32 = jnp.float32
 BF16 = jnp.bfloat16
 CHIPS = 8
+LAST = 6
 CHUNKS = [(d, w) for w in range(3) for d in range(2)]
 
 
@@ -34,8 +36,9 @@
     g, wt, m, v = (refs[i : i + 3] for i in (0, 3, 6, 9))
     x, gsum = refs[12:15], refs[15:18]
     factor_ref = refs[18]
-    (p_gu, p_dn, r_gu, r_dn, o_gu, o_dn, w_gu, w_dn, m_gu, m_dn, v_gu, v_dn, acc, norms) = refs[19:33]
-    (p_send, p_recv, r_send, r_recv, o_sem, state_sem, a_send, a_recv, n_send, n_recv, l_sem, g_sem) = refs[33:]
+    edge_gu, edge_dn = refs[19:21], refs[21:23]
+    (p_gu, p_dn, r_gu, r_dn, o_gu, o_dn, w_gu, w_dn, m_gu, m_dn, v_gu, v_dn, acc, norms) = refs[23:37]
+    (p_send, p_recv, r_send, r_recv, o_sem, state_sem, a_send, a_recv, n_send, n_recv, l_sem, g_sem) = refs[37:]
 
     rep, dp = lax.axis_index("rep"), lax.axis_index("dp")
     y, z, c = dp // 8, (dp // 2) % 4, dp % 2
@@ -190,24 +193,36 @@
     factor_ref[...] = factor
     scale = jnp.broadcast_to(factor[0:1, 0:1], (16, 1024))
 
+    def edge(d, w):
+        return edge_gu[d].at[w] if w < 2 else edge_dn[d]
+
+    def held(h, d, w):
+        if isinstance(h, int) and h == 0:
+            return pick(p_gu, p_dn, (0,), d, w)
+        if isinstance(h, int) and h == LAST:
+            return edge(d, w)
+        return rows_of(x, w, d, device_at(gathered(h, d), c))
+
     def gather_hop(h, d, w):
-        block = device_at(gathered(h, d), c)
-        src = pick(p_gu, p_dn, (0,), d, w) if isinstance(h, int) and h == 0 else rows_of(x, w, d, block)
-        return pltpu.make_async_remote_copy(
-            src, rows_of(x, w, d, block), a_send.at[h, d * 3 + w], a_recv.at[h, d * 3 + w], device_id=nxt[d], device_id_type=MESH
+        dst = edge(d, w) if isinstance(h, int) and h == LAST - 1 else rows_of(x, w, d, device_at(gathered(h, d), c))
+        return pltpu.make_async_remote_copy(
+            held(h, d, w), dst, a_send.at[h, d * 3 + w], a_recv.at[h, d * 3 + w], device_id=nxt[d], device_id_type=MESH
         )
 
     def gather_from(h, d, w):
-        block = rows_of(x, w, d, device_at(gathered(h, d), c))
+        block = held(h, d, w)
         return pltpu.make_async_remote_copy(
             block, block, a_send.at[h - 1, d * 3 + w], a_recv.at[h - 1, d * 3 + w], device_id=nxt[d], device_id_type=MESH
         )
 
     def share(h, d, w):
-        block = device_at(gathered(h, d), c)
-        src = pick(p_gu, p_dn, (0,), d, w) if isinstance(h, int) and h == 0 else rows_of(x, w, d, block)
-        return pltpu.make_async_remote_copy(
-            src, rows_of(x, w, d, block), p_send.at[h, d * 3 + w], p_recv.at[h, d * 3 + w], device_id=partner, device_id_type=MESH
+        return pltpu.make_async_remote_copy(
+            held(h, d, w),
+            rows_of(x, w, d, device_at(gathered(h, d), c)),
+            p_send.at[h, d * 3 + w],
+            p_recv.at[h, d * 3 + w],
+            device_id=partner,
+            device_id_type=MESH,
         )
 
     def shared(h, d, w):
@@ -242,10 +257,11 @@
             share(h, d, w).start()
         return carry
 
-    lax.fori_loop(1, 7, gather_step, 0)
-    for d, w in CHUNKS:
-        gather_from(7, d, w).wait_recv()
-        share(7, d, w).start()
+    lax.fori_loop(1, LAST - 1, gather_step, 0)
+    gather_step(LAST - 1, 0)
+    for d, w in CHUNKS:
+        gather_from(LAST, d, w).wait_recv()
+        share(LAST, d, w).start()
 
     for r in range(1, 16):
         norm_to(r).wait_send()
@@ -258,32 +274,187 @@
             gather_from(h + 1, d, w).wait_send()
         return carry
 
-    lax.fori_loop(0, 7, drain, 0)
+    lax.fori_loop(0, LAST, drain, 0)
 
     def drain_shares(h, carry):
         for d, w in CHUNKS:
             shared(h, d, w).wait()
         return carry
 
-    lax.fori_loop(0, 8, drain_shares, 0)
+    lax.fori_loop(0, LAST + 1, drain_shares, 0)
+
+
+def place():
+    dp = lax.axis_index("dp")
+    y, z, c = dp // 8, (dp // 2) % 4, dp % 2
+    return dp, z + y * (7 - 2 * z), c
+
+
+def block_rows(array, d, dev, count=1):
+    n = array.shape[1] // 16
+    return array.at[d, pl.ds(pl.multiple_of(dev * n, n), n * count)]
+
+
+def from_chip(q, h, d):
+    return (q + CHIPS - h) % CHIPS if d == 0 else (q + h) % CHIPS
+
+
+def arrived(x, edges, out):
+    _, q, c = place()
+    pairs = []
+    for d in range(2):
+        for h in range(LAST):
+            chip = device_at(from_chip(q, h, d), 0)
+            pairs.append((block_rows(x, d, chip, 2), block_rows(out, d, chip, 2)))
+        chip = from_chip(q, LAST, d)
+        pairs.append((edges[d], block_rows(out, d, device_at(chip, c))))
+        other = device_at(chip, 1 - c)
+        pairs.append((block_rows(x, d, other), block_rows(out, d, other)))
+    return pairs
+
+
+def through(pairs, slots, in_sem, out_sem):
+    loads, stores = [], []
+    for i, (src, dst) in enumerate(pairs):
+        at = slots.at[i % 16, pl.ds(0, src.shape[0])]
+        loads.append(pltpu.make_async_copy(src, at, in_sem.at[i % 16]))
+        stores.append(pltpu.make_async_copy(at, dst, out_sem.at[i % 16]))
+    n = len(pairs)
+    for i in range(min(8, n)):
+        loads[i].start()
+    for i in range(n):
+        loads[i].wait()
+        stores[i].start()
+        if i >= 8:
+            stores[i - 8].wait()
+        if i + 8 < n:
+            loads[i + 8].start()
+    for i in range(max(0, n - 8), n):
+        stores[i].wait()
+
+
+def copy_wide(xg, xu, e0, e1, out_g, out_u, slots, in_sem, out_sem):
+    pairs = []
+    for w, (x, out) in enumerate(((xg, out_g), (xu, out_u))):
+        pairs += arrived(x, [e0.at[w], e1.at[w]], out)
+    through(pairs, slots, in_sem, out_sem)
+
+
+def copy_down(*refs):
+    factor, x, e0, e1 = refs[:4]
+    gs, ms, vs = refs[4:7], refs[7:10], refs[10:13]
+    out, m_out, v_out = refs[13], refs[14:17], refs[17:20]
+    slots, g_gu, g_dn, m_gu, m_dn, v_gu, v_dn, in_sem, out_sem, state_in, state_out = refs[20:]
+
+    def pick(gu, dn, d, w):
+        return gu.at[d, w] if w < 2 else dn.at[d]
+
+    def load(d, w):
+        i = d * 3 + w
+        return [
+            pltpu.make_async_copy(gs[w].at[d], pick(g_gu, g_dn, d, w), state_in.at[0, i]),
+            pltpu.make_async_copy(ms[w].at[d], pick(m_gu, m_dn, d, w), state_in.at[1, i]),
+            pltpu.make_async_copy(vs[w].at[d], pick(v_gu, v_dn, d, w), state_in.at[2, i]),
+        ]
+
+    def store(d, w):
+        i = d * 3 + w
+        return [
+            pltpu.make_async_copy(pick(m_gu, m_dn, d, w), m_out[w].at[d], state_out.at[0, i]),
+            pltpu.make_async_copy(pick(v_gu, v_dn, d, w), v_out[w].at[d], state_out.at[1, i]),
+        ]
+
+    for d, w in CHUNKS:
+        for one in load(d, w):
+            one.start()
+    scale = jnp.broadcast_to(factor[0:1, 0:1], (16, 1024))
+    for d, w in CHUNKS:
+        for one in load(d, w):
+            one.wait()
+        gr, mr, vr = pick(g_gu, g_dn, d, w), pick(m_gu, m_dn, d, w), pick(v_gu, v_dn, d, w)
+
+        def update(rows, cols):
+            grad = gr[rows, cols].astype(F32) * scale
+            mr[rows, cols] = 0.9 * mr[rows, cols] + 0.1 * grad
+            vr[rows, cols] = 0.95 * vr[rows, cols] + 0.05 * grad * grad
+
+        tiles(gr, update)
+        for one in store(d, w):
+            one.start()
+    through(arrived(x, [e0, e1], out), slots, in_sem, out_sem)
+    for d, w in CHUNKS:
+        for one in store(d, w):
+            one.wait()
+
+
+def finish(weights, *refs):
+    lands = refs[weights : weights + 4]
+    outs = refs[weights + 4 : 2 * weights + 4]
+    slots, in_sem, out_sem = refs[2 * weights + 4 :]
+    _, q, c = place()
+    pairs = []
+    for d in range(2):
+        chip = from_chip(q, LAST + 1, d)
+        for which in range(2):
+            dev = device_at(chip, c if which == 0 else 1 - c)
+            for w in range(weights):
+                src = lands[which * 2 + d]
+                pairs.append((src.at[w] if weights > 1 else src, block_rows(outs[w], d, dev)))
+    through(pairs, slots, in_sem, out_sem)
 
 
 def solution(mesh):
     whole = [(2, 1024, 4096), (2, 1024, 4096), (2, 4096, 1024)]
     block = [(2, 64, 4096), (2, 64, 4096), (2, 256, 1024)]
 
+    def shapes(dims, dtype):
+        return [jax.ShapeDtypeStruct(s, dtype) for s in dims]
+
     def pair(lead, dtype):
         return [pltpu.VMEM((*lead, 2, 2, 64, 4096), dtype), pltpu.VMEM((*lead, 2, 256, 1024), dtype)]
 
     dma = pltpu.SemaphoreType.DMA
-    any_space = pl.BlockSpec(memory_space=pl.ANY)
+    anywhere = pl.BlockSpec(memory_space=pl.ANY)
+    hbm = pl.BlockSpec(memory_space=pltpu.HBM)
+    vmem = pl.BlockSpec(memory_space=pltpu.VMEM)
+    mib = 1024 * 1024
+
+    def local(body, outs, ins, scratch, moved, aliases=None, specs=None):
+        return call_local(body, outs, ins, scratch, moved, aliases, specs)
+
+    def call_local(body, outs, ins, scratch, moved, aliases, specs):
+        return pl.pallas_call(
+            body,
+            out_shape=outs,
+            in_specs=specs or [hbm] * len(ins),
+            out_specs=[hbm] * len(outs),
+            scratch_shapes=scratch,
+            input_output_aliases=aliases or {},
+            cost_estimate=pl.CostEstimate(flops=int(moved * 40), bytes_accessed=int(moved), transcendentals=0),
+            compiler_params=pltpu.CompilerParams(vmem_limit_bytes=48 * mib),
+        )(*ins)
+
+    def permute(array, pairs):
+        return lax.ppermute(array, "dp", pairs)
+
+    def at(q, c):
+        return device_at(q % CHIPS, c)
+
+    clockwise = [(at(q, c), at(q + 1, c)) for q in range(CHIPS) for c in range(2)]
+    ways = [clockwise, [(b, a) for a, b in clockwise]]
+    across = [(i, i ^ 1) for i in range(16)]
 
     def step(*arrays):
+        m, v = arrays[6:9], arrays[9:12]
         out = pl.pallas_call(
             kernel,
-            out_shape=[jax.ShapeDtypeStruct(s, BF16) for s in whole + block] + [jax.ShapeDtypeStruct((8, 128), F32)],
-            in_specs=[any_space] * 12,
-            out_specs=[any_space] * 6 + [pl.BlockSpec(memory_space=pltpu.VMEM)],
+            out_shape=[
+                *shapes(whole + block, BF16),
+                jax.ShapeDtypeStruct((8, 128), F32),
+                *shapes([(2, 64, 4096)] * 2 + [(256, 1024)] * 2, BF16),
+            ],
+            in_specs=[hbm] * 12,
+            out_specs=[hbm] * 6 + [vmem] + [hbm] * 4,
             scratch_shapes=[
                 *pair((8,), BF16),
                 *pair((3,), BF16),
@@ -299,10 +470,45 @@
             compiler_params=pltpu.CompilerParams(collective_id=0, has_side_effects=True, vmem_limit_bytes=66 * 1000 * 1000),
             name="step",
         )(*arrays)
-        new_w, sums, factor = out[:3], out[3:6], out[6][0, 0]
-        m, v = arrays[6:9], arrays[9:12]
-        gs = [s.astype(F32) * factor for s in sums]
-        return (*new_w, *(0.9 * a + 0.1 * b for a, b in zip(m, gs)), *(0.95 * a + 0.05 * b * b for a, b in zip(v, gs)))
+        (xg, xu, xd), sums, factor, (e0, e1, f0, f1) = out[:3], out[3:6], out[6], out[7:]
+        wide = [permute(e, ways[d]) for d, e in enumerate((e0, e1))]
+        deep = [permute(e, ways[d]) for d, e in enumerate((f0, f1))]
+        slots = [dma((16,)), dma((16,))]
+        new_g, new_u = local(
+            copy_wide, shapes(whole[:2], BF16), (xg, xu, e0, e1), [pltpu.VMEM((16, 128, 4096), BF16), *slots], 56 * mib
+        )
+        wide += [permute(e, across) for e in wide]
+        new_d, *state = local(
+            copy_down,
+            shapes(whole[2:], BF16) + shapes(block * 2, F32),
+            (factor, xd, f0, f1, *sums, *m, *v),
+            [
+                pltpu.VMEM((16, 512, 1024), BF16), *pair((), BF16), *pair((), F32), *pair((), F32),
+                *slots, dma((3, 6)), dma((2, 6)),
+            ],
+            56 * mib,
+            specs=[vmem] + [hbm] * 12,
+        )
+        deep += [permute(e, across) for e in deep]
+        new_g, new_u = local(
+            lambda *refs: finish(2, *refs),
+            shapes(whole[:2], BF16),
+            (new_g, new_u, *wide),
+            [pltpu.VMEM((16, 64, 4096), BF16), *slots],
+            8 * mib,
+            {0: 0, 1: 1},
+            [hbm] * 2 + [anywhere] * 4,
+        )
+        (new_d,) = local(
+            lambda *refs: finish(1, *refs),
+            shapes(whole[2:], BF16),
+            (new_d, *deep),
+            [pltpu.VMEM((16, 256, 1024), BF16), *slots],
+            4 * mib,
+            {0: 0},
+            [hbm] + [anywhere] * 4,
+        )
+        return (new_g, new_u, new_d, *state)
 
     all_of, cut = P(None, None, None), P(None, "dp", None)
     return jax.shard_map(

time: 542 us -> 546 us (level)
  waiting for transfers between devices: 0 us -> 33.8 us
  local copies, waits for them, and re-layouts: 34.1 us -> 3.32 us
  other arithmetic: 13.3 us -> 0 us
  Pallas kernels: 494 us -> 504 us
    ppermute x0 -> x8, waiting for transfers between devices: none -> 33.8 us  [permute(): return lax.ppermute(array, 'dp', pairs)]
    unnamed x25 -> x16, local copies, waits for them, and re-layouts: 32.9 us -> 3.32 us
    add x2 -> x0, other arithmetic: 13.3 us -> none  [step(): 0.95 * a + 0.05 * b * b]
    pallas_call x1 -> x5, Pallas kernels: 494 us -> 504 us  [the longest x1 461 us: step(): pl.pallas_call(kernel, out_shape=[*shapes(whole + block, BF16), jax.Shape...]
  transfers between devices with their start and end apart: 0 -> 8, of which waited for: 0 -> 4; matrix products, arithmetic and copies ran while one was open for 0% -> 0% of each run, Pallas kernels for 0% -> 7%
where the time goes in v2:
time: 546 us
  Pallas kernels  504 us (92%)
  waiting for transfers between devices  33.8 us (6%)
    pallas_call x1, Pallas kernels, step(): pl.pallas_call(kernel, out_shape=[*shapes(whole + block, BF16), jax.Shape...  461 us
    pallas_call x4, Pallas kernels, call_local(): pl.pallas_call(body, out_shape=outs, in_specs=specs or [hbm] * len(ins),...  42.9 us
    ppermute x8, waiting for transfers between devices, permute(): return lax.ppermute(array, 'dp', pairs)  33.8 us
  transfers between devices with their start and end apart: 8, of which 4 were waited for; matrix products, arithmetic and copies ran while one was open for 0% of the time, Pallas kernels for 7%

profile of v2, /device:TPU:0, one launch (start us, length us, event | category | flops | bytes accessed | tf_op | source)
XLA Modules:
  0.0 545.5 jit_solution(14307411555752484559)
XLA Ops:
  0.6 460.6 %step.1 = (bf16[2,1024,4096]{2,1,0:T(8,128)(2,1)}, bf16[2,1024,4096]{2,1,0:T(8,128)(2,1)}, bf16[2,4096,1024]{2,1,0:T(8,128)(2,1)}, bf16[2,64,4096]{2,1,0:T(8,128...) custom-call(bf16[1,2,1024,4096]{3,2,1,0:T(8,128)(2,1)} %refs_0_.1, ...), custom_call_target="tpu_custom_call" | custom-call | tf_op jit(solution)/shard_map/step/pallas_call | solution.py:449
  461.3 1.3 collective-permute-start
  462.6 0.8 collective-permute-start.1
  463.4 1.2 collective-permute-start.4
  464.6 0.8 collective-permute-start.5
  465.4 22.2 %collective-permute-done.refs_2_ = bf16[2,64,4096]{2,1,0:T(8,128)(2,1)S(1)} collective-permute-done((bf16[2,64,4096]{2,1,0:T(8,128)(2,1)}, bf16[2,64,4096]{2,1,0:T(8,128)(2,1)S(1)}, u32[]{:S(2)}, u32[]{:S(2)}) %collective-permute-start) | collective-permute-done | bytes 1048608 | tf_op jit(solution)/shard_map/ppermute | solution.py:438
  487.6 0.0 collective-permute-start.2
  487.6 1.2 collective-permute-done.1.refs_3_
  488.8 9.4 %collective-permute-done.4.refs_1_ = bf16[256,1024]{1,0:T(8,128)(2,1)S(1)} collective-permute-done((bf16[256,1024]{1,0:T(8,128)(2,1)}, bf16[256,1024]{1,0:T(8,128)(2,1)S(1)}, u32[]{:S(2)}, u32[]{:S(2)}) %collective-permute-start.4) | collective-permute-done | bytes 524320 | tf_op jit(solution)/shard_map/ppermute | solution.py:438
  498.2 0.9 collective-permute-done.5.refs_2_
  499.2 0.0 collective-permute-start.7
  499.2 1.2 copy-done.3
  500.4 1.2 copy-done.4
  501.6 19.3 %shard_map.187 = (bf16[2,1024,4096]{2,1,0:T(8,128)(2,1)}, bf16[2,1024,4096]{2,1,0:T(8,128)(2,1)}) custom-call(bf16[2,1024,4096]{2,1,0:T(8,128)(2,1)} %get-tuple-element.31.xg, bf16[2,1024,4096]{2,1,0:T(8,128)(2,1)} %get-tuple-element.32.xu, bf16[2,64,4096]{2,1,0:T(8,128)(2,1)S(1)} %copy-done.3, bf16[2,64,4096]{2,1,0:T(8,128)(2,1)S(1)} %copy-done.4), custom_call_target="tpu_custom_call" | custom-call | flops 2348810240 | bytes 58720256 | tf_op jit(solution)/shard_map/pallas_call | solution.py:426
  521.0 0.0 copy-done.1
  521.0 0.6 copy-done.2
  521.5 0.1 copy-done.5
  521.7 0.2 copy-done.6
  521.8 19.2 %shard_map.189 = (bf16[2,4096,1024]{2,1,0:T(8,128)(2,1)}, f32[2,64,4096]{2,1,0:T(8,128)}, f32[2,64,4096]{2,1,0:T(8,128)}, f32[2,256,1024]{2,1,0:T(8,128)}, f32[2...) custom-call(f32[8,128]{1,0:T(8,128)S(1)} %copy-done.7, ...), custom_call_target="tpu_custom_call" | custom-call | flops 2348810240 | bytes 58720256 | tf_op jit(solution)/shard_map/pallas_call | solution.py:426
  541.1 0.0 collective-permute-done.6.refs_3_
  541.1 0.0 collective-permute-done.7.refs_4_
  541.1 1.8 shard_map.190
  542.9 0.0 collective-permute-done.2.refs_4_
  542.9 2.6 shard_map.188
  (13 shorter events, 0.0 us)
Async XLA Ops:
  461.3 26.3 %collective-permute-start = (bf16[2,64,4096]{2,1,0:T(8,128)(2,1)}, bf16[2,64,4096]{2,1,0:T(8,128)(2,1)S(1)}, u32[]{:S(2)}, u32[]{:S(2)}) collective-permute-start(bf16[2,64,4096]{2,1,0:T(8,128)(2,1)} %get-tuple-element.33.e0), channel_id=1, source_target_pairs={{0,2},{1,3},{2,4},{3,5},{4,6},{5,7},{6,14},{7,15},{14,12},{15,13},... | collective-permute-start | bytes 3145736 | tf_op jit(solution)/shard_map/ppermute | solution.py:438
  462.6 26.2 %collective-permute-start.1 = (bf16[2,64,4096]{2,1,0:T(8,128)(2,1)}, bf16[2,64,4096]{2,1,0:T(8,128)(2,1)S(1)}, u32[]{:S(2)}, u32[]{:S(2)}) collective-permute-start(bf16[2,64,4096]{2,1,0:T(8,128)(2,1)} %get-tuple-element.34.e1), channel_id=1, source_target_pairs={{2,0},{3,1},{4,2},{5,3},{6,4},{7,5},{14,6},{15,7},{12,14},{13,15},... | collective-permute-start | bytes 3145736 | tf_op jit(solution)/shard_map/ppermute | solution.py:438
  463.4 34.9 %collective-permute-start.4 = (bf16[256,1024]{1,0:T(8,128)(2,1)}, bf16[256,1024]{1,0:T(8,128)(2,1)S(1)}, u32[]{:S(2)}, u32[]{:S(2)}) collective-permute-start(bf16[256,1024]{1,0:T(8,128)(2,1)} %get-tuple-element.41.refs_2_), channel_id=1, source_target_pairs={{0,2},{1,3},{2,4},{3,5},{4,6},{5,7},{6,14},{7,15},{14,12},{15,13},... | collective-permute-start | bytes 1572872 | tf_op jit(solution)/shard_map/ppermute | solution.py:438
  464.6 34.6 %collective-permute-start.5 = (bf16[256,1024]{1,0:T(8,128)(2,1)}, bf16[256,1024]{1,0:T(8,128)(2,1)S(1)}, u32[]{:S(2)}, u32[]{:S(2)}) collective-permute-start(bf16[256,1024]{1,0:T(8,128)(2,1)} %get-tuple-element.42.refs_3_), channel_id=1, source_target_pairs={{2,0},{3,1},{4,2},{5,3},{6,4},{7,5},{14,6},{15,7},{12,14},{13,15},... | collective-permute-start | bytes 1572872 | tf_op jit(solution)/shard_map/ppermute | solution.py:438
  487.6 55.3 %collective-permute-start.2 = (bf16[2,64,4096]{2,1,0:T(8,128)(2,1)S(1)}, bf16[2,64,4096]{2,1,0:T(8,128)(2,1)S(1)}, u32[]{:S(2)}, u32[]{:S(2)}) collective-permute-start(bf16[2,64,4096]{2,1,0:T(8,128)(2,1)S(1)} %collective-permute-done.refs_2_), channel_id=1, source_target_pairs={{0,1},{1,0},{2,3},{3,2},{4,5},{5,4},{6,7},{7,6},{8,9},{9,8},{10,11... | collective-permute-start | bytes 3145736 | tf_op jit(solution)/shard_map/ppermute | solution.py:438
  488.8 54.1 %collective-permute-start.3 = (bf16[2,64,4096]{2,1,0:T(8,128)(2,1)S(1)}, bf16[2,64,4096]{2,1,0:T(8,128)(2,1)S(1)}, u32[]{:S(2)}, u32[]{:S(2)}) collective-permute-start(bf16[2,64,4096]{2,1,0:T(8,128)(2,1)S(1)} %collective-permute-done.1.refs_3_), channel_id=1, source_target_pairs={{0,1},{1,0},{2,3},{3,2},{4,5},{5,4},{6,7},{7,6},{8,9},{9,8},{10,11... | collective-permute-start | bytes 3145736 | tf_op jit(solution)/shard_map/ppermute | solution.py:438
  498.2 42.8 %collective-permute-start.6 = (bf16[256,1024]{1,0:T(8,128)(2,1)S(1)}, bf16[256,1024]{1,0:T(8,128)(2,1)S(1)}, u32[]{:S(2)}, u32[]{:S(2)}) collective-permute-start(bf16[256,1024]{1,0:T(8,128)(2,1)S(1)} %collective-permute-done.4.refs_1_), channel_id=1, source_target_pairs={{0,1},{1,0},{2,3},{3,2},{4,5},{5,4},{6,7},{7,6},{8,9},{9,8},{10,11... | collective-permute-start | bytes 1572872 | tf_op jit(solution)/shard_map/ppermute | solution.py:438
  499.2 41.9 %collective-permute-start.7 = (bf16[256,1024]{1,0:T(8,128)(2,1)S(1)}, bf16[256,1024]{1,0:T(8,128)(2,1)S(1)}, u32[]{:S(2)}, u32[]{:S(2)}) collective-permute-start(bf16[256,1024]{1,0:T(8,128)(2,1)S(1)} %collective-permute-done.5.refs_2_), channel_id=1, source_target_pairs={{0,1},{1,0},{2,3},{3,2},{4,5},{5,4},{6,7},{7,6},{8,9},{9,8},{10,11... | collective-permute-start | bytes 1572872 | tf_op jit(solution)/shard_map/ppermute | solution.py:438
  499.2 1.2 copy-start.3
  500.4 1.2 copy-start.4
  501.6 19.3 %copy-start = (bf16[2,64,4096]{2,1,0:T(8,128)(2,1)S(1)}, bf16[2,64,4096]{2,1,0:T(8,128)(2,1)}, u32[]{:S(2)}) copy-start(bf16[2,64,4096]{2,1,0:T(8,128)(2,1)} %get-tuple-element.43.refs_4_) | copy-start | bytes 3145732
  501.6 19.4 %copy-start.1 = (bf16[2,64,4096]{2,1,0:T(8,128)(2,1)S(1)}, bf16[2,64,4096]{2,1,0:T(8,128)(2,1)}, u32[]{:S(2)}) copy-start(bf16[2,64,4096]{2,1,0:T(8,128)(2,1)} %get-tuple-element.44.refs_5_) | copy-start | bytes 3145732
  501.6 19.9 %copy-start.2 = (bf16[2,256,1024]{2,1,0:T(8,128)(2,1)S(1)}, bf16[2,256,1024]{2,1,0:T(8,128)(2,1)}, u32[]{:S(2)}) copy-start(bf16[2,256,1024]{2,1,0:T(8,128)(2,1)} %get-tuple-element.45.refs_6_) | copy-start | bytes 3145732
  501.6 20.1 %copy-start.5 = (bf16[256,1024]{1,0:T(8,128)(2,1)S(1)}, bf16[256,1024]{1,0:T(8,128)(2,1)}, u32[]{:S(2)}) copy-start(bf16[256,1024]{1,0:T(8,128)(2,1)} %get-tuple-element.41.refs_2_) | copy-start | bytes 1572868
  501.6 20.2 %copy-start.6 = (bf16[256,1024]{1,0:T(8,128)(2,1)S(1)}, bf16[256,1024]{1,0:T(8,128)(2,1)}, u32[]{:S(2)}) copy-start(bf16[256,1024]{1,0:T(8,128)(2,1)} %get-tuple-element.42.refs_3_) | copy-start | bytes 1572868
  501.6 20.2 %copy-start.7 = (f32[8,128]{1,0:T(8,128)S(1)}, f32[8,128]{1,0:T(8,128)}, u32[]{:S(2)}) copy-start(f32[8,128]{1,0:T(8,128)} %get-tuple-element.39.refs_0_) | copy-start | bytes 12292

commit v3 on v2

--- a/solution.py
+++ b/solution.py
@@ -10,7 +10,7 @@
 F32 = jnp.float32
 BF16 = jnp.bfloat16
 CHIPS = 8
-LAST = 6
+LAST = 5
 CHUNKS = [(d, w) for w in range(3) for d in range(2)]
 
 
@@ -261,7 +261,6 @@
     gather_step(LAST - 1, 0)
     for d, w in CHUNKS:
         gather_from(LAST, d, w).wait_recv()
-        share(LAST, d, w).start()
 
     for r in range(1, 16):
         norm_to(r).wait_send()
@@ -281,7 +280,7 @@
             shared(h, d, w).wait()
         return carry
 
-    lax.fori_loop(0, LAST + 1, drain_shares, 0)
+    lax.fori_loop(0, LAST, drain_shares, 0)
 
 
 def place():
@@ -299,17 +298,19 @@
     return (q + CHIPS - h) % CHIPS if d == 0 else (q + h) % CHIPS
 
 
-def arrived(x, edges, out):
+def arrived(x, out):
+    _, q, _ = place()
+    chips = [(d, device_at(from_chip(q, h, d), 0)) for d in range(2) for h in range(LAST)]
+    return [(block_rows(x, d, chip, 2), block_rows(out, d, chip, 2)) for d, chip in chips]
+
+
+def landed(hop, lands, outs):
     _, q, c = place()
     pairs = []
-    for d in range(2):
-        for h in range(LAST):
-            chip = device_at(from_chip(q, h, d), 0)
-            pairs.append((block_rows(x, d, chip, 2), block_rows(out, d, chip, 2)))
-        chip = from_chip(q, LAST, d)
-        pairs.append((edges[d], block_rows(out, d, device_at(chip, c))))
-        other = device_at(chip, 1 - c)
-        pairs.append((block_rows(x, d, other), block_rows(out, d, other)))
+    for i, land in enumerate(lands):
+        dev = device_at(from_chip(q, hop, i % 2), c if i < 2 else 1 - c)
+        for w, out in enumerate(outs):
+            pairs.append((land.at[w] if len(outs) > 1 else land, block_rows(out, i % 2, dev)))
     return pairs
 
 
@@ -333,18 +334,15 @@
         stores[i].wait()
 
 
-def copy_wide(xg, xu, e0, e1, out_g, out_u, slots, in_sem, out_sem):
-    pairs = []
-    for w, (x, out) in enumerate(((xg, out_g), (xu, out_u))):
-        pairs += arrived(x, [e0.at[w], e1.at[w]], out)
-    through(pairs, slots, in_sem, out_sem)
+def copy_wide(xg, xu, out_g, out_u, slots, in_sem, out_sem):
+    through(arrived(xg, out_g) + arrived(xu, out_u), slots, in_sem, out_sem)
 
 
 def copy_down(*refs):
-    factor, x, e0, e1 = refs[:4]
-    gs, ms, vs = refs[4:7], refs[7:10], refs[10:13]
-    out, m_out, v_out = refs[13], refs[14:17], refs[17:20]
-    slots, g_gu, g_dn, m_gu, m_dn, v_gu, v_dn, in_sem, out_sem, state_in, state_out = refs[20:]
+    factor, x = refs[:2]
+    gs, ms, vs = refs[2:5], refs[5:8], refs[8:11]
+    out, m_out, v_out = refs[11], refs[12:15], refs[15:18]
+    slots, g_gu, g_dn, m_gu, m_dn, v_gu, v_dn, in_sem, out_sem, state_in, state_out = refs[18:]
 
     def pick(gu, dn, d, w):
         return gu.at[d, w] if w < 2 else dn.at[d]
@@ -381,26 +379,27 @@
         tiles(gr, update)
         for one in store(d, w):
             one.start()
-    through(arrived(x, [e0, e1], out), slots, in_sem, out_sem)
+    through(arrived(x, out), slots, in_sem, out_sem)
     for d, w in CHUNKS:
         for one in store(d, w):
             one.wait()
 
 
+def settle(*refs):
+    lands, outs, (wide_slots, down_slots, in_sem, out_sem) = refs[3:19], refs[19:22], refs[22:]
+    wide = landed(LAST, lands[0:4], outs[:2]) + landed(LAST + 1, lands[4:8], outs[:2])
+    down = landed(LAST, lands[8:12], outs[2:]) + landed(LAST + 1, lands[12:16], outs[2:])
+    through(wide, wide_slots, in_sem, out_sem)
+    through(down, down_slots, in_sem, out_sem)
+
+
 def finish(weights, *refs):
-    lands = refs[weights : weights + 4]
-    outs = refs[weights + 4 : 2 * weights + 4]
-    slots, in_sem, out_sem = refs[2 * weights + 4 :]
-    _, q, c = place()
-    pairs = []
-    for d in range(2):
-        chip = from_chip(q, LAST + 1, d)
-        for which in range(2):
-            dev = device_at(chip, c if which == 0 else 1 - c)
-            for w in range(weights):
-                src = lands[which * 2 + d]
-                pairs.append((src.at[w] if weights > 1 else src, block_rows(outs[w], d, dev)))
-    through(pairs, slots, in_sem, out_sem)
+    lands, outs, sem = refs[weights : weights + 4], refs[weights + 4 : 2 * weights + 4], refs[-1]
+    copies = [pltpu.make_async_copy(src, dst, sem.at[i]) for i, (src, dst) in enumerate(landed(LAST + 2, lands, outs))]
+    for copy in copies:
+        copy.start()
+    for copy in copies:
+        copy.wait()
 
 
 def solution(mesh):
@@ -419,10 +418,10 @@
     vmem = pl.BlockSpec(memory_space=pltpu.VMEM)
     mib = 1024 * 1024
 
-    def local(body, outs, ins, scratch, moved, aliases=None, specs=None):
-        return call_local(body, outs, ins, scratch, moved, aliases, specs)
-
-    def call_local(body, outs, ins, scratch, moved, aliases, specs):
+    def local(body, outs, ins, scratch, moved, limit, aliases=None, specs=None):
+        return call_local(body, outs, ins, scratch, moved, limit, aliases, specs)
+
+    def call_local(body, outs, ins, scratch, moved, limit, aliases, specs):
         return pl.pallas_call(
             body,
             out_shape=outs,
@@ -431,7 +430,7 @@
             scratch_shapes=scratch,
             input_output_aliases=aliases or {},
             cost_estimate=pl.CostEstimate(flops=int(moved * 40), bytes_accessed=int(moved), transcendentals=0),
-            compiler_params=pltpu.CompilerParams(vmem_limit_bytes=48 * mib),
+            compiler_params=pltpu.CompilerParams(vmem_limit_bytes=limit * mib),
         )(*ins)
 
     def permute(array, pairs):
@@ -471,42 +470,53 @@
             name="step",
         )(*arrays)
         (xg, xu, xd), sums, factor, (e0, e1, f0, f1) = out[:3], out[3:6], out[6], out[7:]
-        wide = [permute(e, ways[d]) for d, e in enumerate((e0, e1))]
-        deep = [permute(e, ways[d]) for d, e in enumerate((f0, f1))]
         slots = [dma((16,)), dma((16,))]
+
+        def hop_on(arrays):
+            return [permute(e, ways[d]) for d, e in enumerate(arrays)]
+
+        def cross(arrays):
+            return [permute(e, across) for e in arrays]
+
+        wide5, deep5 = [e0, e1], [f0, f1]
+        wide6, deep6 = hop_on(wide5), hop_on(deep5)
+        their_wide5, their_deep5 = cross(wide5), cross(deep5)
         new_g, new_u = local(
-            copy_wide, shapes(whole[:2], BF16), (xg, xu, e0, e1), [pltpu.VMEM((16, 128, 4096), BF16), *slots], 56 * mib
-        )
-        wide += [permute(e, across) for e in wide]
+            copy_wide, shapes(whole[:2], BF16), (xg, xu), [pltpu.VMEM((16, 128, 4096), BF16), *slots], 40 * mib, 50
+        )
+        wide7, their_wide6 = hop_on(wide6), cross(wide6)
         new_d, *state = local(
             copy_down,
             shapes(whole[2:], BF16) + shapes(block * 2, F32),
-            (factor, xd, f0, f1, *sums, *m, *v),
+            (factor, xd, *sums, *m, *v),
             [
                 pltpu.VMEM((16, 512, 1024), BF16), *pair((), BF16), *pair((), F32), *pair((), F32),
                 *slots, dma((3, 6)), dma((2, 6)),
             ],
-            56 * mib,
-            specs=[vmem] + [hbm] * 12,
-        )
-        deep += [permute(e, across) for e in deep]
+            48 * mib,
+            50,
+            specs=[vmem] + [hbm] * 10,
+        )
+        deep7, their_deep6 = hop_on(deep6), cross(deep6)
+        news = local(
+            settle,
+            shapes(whole, BF16),
+            (new_g, new_u, new_d, *wide5, *their_wide5, *wide6, *their_wide6, *deep5, *their_deep5, *deep6, *their_deep6),
+            [pltpu.VMEM((16, 64, 4096), BF16), pltpu.VMEM((16, 256, 1024), BF16), *slots],
+            24 * mib,
+            24,
+            {0: 0, 1: 1, 2: 2},
+            [hbm] * 3 + [anywhere] * 16,
+        )
+        their_wide7 = cross(wide7)
         new_g, new_u = local(
-            lambda *refs: finish(2, *refs),
-            shapes(whole[:2], BF16),
-            (new_g, new_u, *wide),
-            [pltpu.VMEM((16, 64, 4096), BF16), *slots],
-            8 * mib,
-            {0: 0, 1: 1},
-            [hbm] * 2 + [anywhere] * 4,
-        )
+            lambda *refs: finish(2, *refs), shapes(whole[:2], BF16), (*news[:2], *wide7, *their_wide7), [dma((8,))],
+            8 * mib, 24, {0: 0, 1: 1}, [hbm] * 2 + [anywhere] * 4,
+        )
+        their_deep7 = cross(deep7)
         (new_d,) = local(
-            lambda *refs: finish(1, *refs),
-            shapes(whole[2:], BF16),
-            (new_d, *deep),
-            [pltpu.VMEM((16, 256, 1024), BF16), *slots],
-            4 * mib,
-            {0: 0},
-            [hbm] + [anywhere] * 4,
+            lambda *refs: finish(1, *refs), shapes(whole[2:], BF16), (news[2], *deep7, *their_deep7), [dma((8,))],
+            4 * mib, 24, {0: 0}, [hbm] + [anywhere] * 4,
         )
         return (new_g, new_u, new_d, *state)
 

time: 546 us -> 688 us (1.26)
  Pallas kernels: 504 us -> 593 us
  waiting for transfers between devices: 33.8 us -> 70.2 us
  local copies, waits for them, and re-layouts: 3.32 us -> 12.6 us
    pallas_call x4 -> x5, Pallas kernels: 42.9 us -> 168 us  [call_local(): pl.pallas_call(body, out_shape=outs, in_specs=specs or [hbm] * len(ins),...]
    ppermute x8 -> x20, waiting for transfers between devices: 33.8 us -> 70.2 us  [permute(): return lax.ppermute(array, 'dp', pairs)]
    pallas_call x1, Pallas kernels: 461 us -> 425 us  [step(): pl.pallas_call(kernel, out_shape=[*shapes(whole + block, BF16), jax.Shape...]
    unnamed x16 -> x40, local copies, waits for them, and re-layouts: 3.32 us -> 12.6 us
  transfers between devices with their start and end apart: 8 -> 20, of which waited for: 4 -> 6; matrix products, arithmetic and copies ran while one was open for 0% -> 0% of each run, Pallas kernels for 7% -> 15%
where the time goes in v3:
time: 688 us; the launch traced here: 687 us
  Pallas kernels  593 us (86%)
  waiting for transfers between devices  70.2 us (10%)
  local copies, waits for them, and re-layouts  12.6 us (2%)
  starting transfers between devices  10.4 us (2%)
    pallas_call x1, Pallas kernels, step(): pl.pallas_call(kernel, out_shape=[*shapes(whole + block, BF16), jax.Shape...  425 us
    pallas_call x5, Pallas kernels, call_local(): pl.pallas_call(body, out_shape=outs, in_specs=specs or [hbm] * len(ins),...  168 us
    ppermute x20, waiting for transfers between devices, permute(): return lax.ppermute(array, 'dp', pairs)  70.2 us
  transfers between devices with their start and end apart: 20, of which 6 were waited for; matrix products, arithmetic and copies ran while one was open for 0% of the time, Pallas kernels for 15%

profile of v3, /device:TPU:0, one launch (start us, length us, event | category | flops | bytes accessed | tf_op | source)
XLA Modules:
  0.0 687.3 jit_solution(13671838402430021456)
XLA Ops:
  0.6 425.0 %step.1 = (bf16[2,1024,4096]{2,1,0:T(8,128)(2,1)}, bf16[2,1024,4096]{2,1,0:T(8,128)(2,1)}, bf16[2,4096,1024]{2,1,0:T(8,128)(2,1)}, bf16[2,64,4096]{2,1,0:T(8,128...) custom-call(bf16[1,2,1024,4096]{3,2,1,0:T(8,128)(2,1)} %refs_0_.1, ...), custom_call_target="tpu_custom_call" | custom-call | tf_op jit(solution)/shard_map/step/pallas_call | solution.py:448
  426.4 1.4 collective-permute-start.2
  428.4 1.3 collective-permute-start.3
  429.8 10.9 %collective-permute-done.8.refs_15_ = bf16[256,1024]{1,0:T(8,128)(2,1)S(1)} collective-permute-done((bf16[256,1024]{1,0:T(8,128)(2,1)}, bf16[256,1024]{1,0:T(8,128)(2,1)S(1)}, u32[]{:S(2)}, u32[]{:S(2)}) %collective-permute-start.8) | collective-permute-done | bytes 524320 | tf_op jit(solution)/shard_map/ppermute | solution.py:437
  440.7 2.2 collective-permute-done.9.refs_16_
  445.0 16.7 %collective-permute-done.2.refs_7_ = bf16[2,64,4096]{2,1,0:T(8,128)(2,1)S(1)} collective-permute-done((bf16[2,64,4096]{2,1,0:T(8,128)(2,1)}, bf16[2,64,4096]{2,1,0:T(8,128)(2,1)S(1)}, u32[]{:S(2)}, u32[]{:S(2)}) %collective-permute-start.2) | collective-permute-done | bytes 1048608 | tf_op jit(solution)/shard_map/ppermute | solution.py:437
  461.7 1.6 collective-permute-done.3.refs_8_
  463.4 0.9 collective-permute-start.12
  465.0 1.2 collective-permute-start.13
  469.2 29.4 %collective-permute-done.16.refs_1_ = bf16[256,1024]{1,0:T(8,128)(2,1)} collective-permute-done((bf16[256,1024]{1,0:T(8,128)(2,1)S(1)}, bf16[256,1024]{1,0:T(8,128)(2,1)}, u32[]{:S(2)}, u32[]{:S(2)}) %collective-permute-start.16) | collective-permute-done | bytes 524320 | tf_op jit(solution)/shard_map/ppermute | solution.py:437
  498.7 1.4 collective-permute-start.17
  501.4 9.3 %collective-permute-done.17.refs_2_ = bf16[256,1024]{1,0:T(8,128)(2,1)} collective-permute-done((bf16[256,1024]{1,0:T(8,128)(2,1)S(1)}, bf16[256,1024]{1,0:T(8,128)(2,1)}, u32[]{:S(2)}, u32[]{:S(2)}) %collective-permute-start.17) | collective-permute-done | bytes 524320 | tf_op jit(solution)/shard_map/ppermute | solution.py:437
  511.2 14.9 %shard_map.187 = (bf16[2,1024,4096]{2,1,0:T(8,128)(2,1)}, bf16[2,1024,4096]{2,1,0:T(8,128)(2,1)}) custom-call(bf16[2,1024,4096]{2,1,0:T(8,128)(2,1)} %get-tuple-element.34.xg, bf16[2,1024,4096]{2,1,0:T(8,128)(2,1)} %get-tuple-element.35.xu), custom_call_target="tpu_custom_call" | custom-call | flops 1677721600 | bytes 41943040 | tf_op jit(solution)/shard_map/pallas_call | solution.py:425
  526.5 17.8 %shard_map.188 = (bf16[2,4096,1024]{2,1,0:T(8,128)(2,1)}, f32[2,64,4096]{2,1,0:T(8,128)}, f32[2,64,4096]{2,1,0:T(8,128)}, f32[2,256,1024]{2,1,0:T(8,128)}, f32[2...) custom-call(f32[8,128]{1,0:T(8,128)S(1)} %copy-done.19, ...), custom_call_target="tpu_custom_call" | custom-call | flops 2013265920 | bytes 50331648 | tf_op jit(solution)/shard_map/pallas_call | solution.py:425
  544.4 1.0 copy-done.6
  545.4 1.0 copy-done.8
  546.4 1.0 copy-done.10
  547.5 1.0 copy-done.12
  548.5 1.0 copy-done.14
  549.6 1.0 copy-done.16
  550.6 1.0 copy-done.18
  551.6 6.1 shard_map.189
  557.8 64.7 %shard_map.191 = bf16[2,4096,1024]{2,1,0:T(8,128)(2,1)} custom-call(bf16[2,4096,1024]{2,1,0:T(8,128)(2,1)} %get-tuple-element.52.refs_0_, bf16[256,1024]{1,0:T(8,128)(2,1)} %collective-permute-done.16.refs_1_, bf16[256,1024]{1,0:T(8,128)(2,1)} %collective-permute-done.17.refs_2_, ...), custom_call_target="tpu_custom_call", output_to_operand_aliasing={{}: (0, {})} | custom-call | flops 167772160 | bytes 4194304 | tf_op jit(solution)/shard_map/pallas_call | solution.py:425
  622.6 64.8 %shard_map.190 = (bf16[2,1024,4096]{2,1,0:T(8,128)(2,1)}, bf16[2,1024,4096]{2,1,0:T(8,128)(2,1)}) custom-call(bf16[2,1024,4096]{2,1,0:T(8,128)(2,1)} %get-tuple-element.48.refs_0_, bf16[2,1024,4096]{2,1,0:T(8,128)(2,1)} %get-tuple-element.49.refs_1_, ...), custom_call_target="tpu_custom_call", output_to_operand_aliasing={{0}: (0, {}), {1}: (1, {})} | custom-call | flops 335544320 | bytes 8388608 | tf_op jit(solution)/shard_map/pallas_call | solution.py:425
  (62 shorter events, 9.6 us)
Async XLA Ops:
  425.6 15.1 %collective-permute-start.8 = (bf16[256,1024]{1,0:T(8,128)(2,1)}, bf16[256,1024]{1,0:T(8,128)(2,1)S(1)}, u32[]{:S(2)}, u32[]{:S(2)}) collective-permute-start(bf16[256,1024]{1,0:T(8,128)(2,1)} %get-tuple-element.46.refs_11_), channel_id=1, source_target_pairs={{0,2},{1,3},{2,4},{3,5},{4,6},{5,7},{6,14},{7,15},{14,12},{15,13},... | collective-permute-start | bytes 1572872 | tf_op jit(solution)/shard_map/ppermute | solution.py:437
  426.4 35.3 %collective-permute-start.2 = (bf16[2,64,4096]{2,1,0:T(8,128)(2,1)}, bf16[2,64,4096]{2,1,0:T(8,128)(2,1)S(1)}, u32[]{:S(2)}, u32[]{:S(2)}) collective-permute-start(bf16[2,64,4096]{2,1,0:T(8,128)(2,1)} %get-tuple-element.44.refs_3_), channel_id=1, source_target_pairs={{0,2},{1,3},{2,4},{3,5},{4,6},{5,7},{6,14},{7,15},{14,12},{15,13},... | collective-permute-start | bytes 3145736 | tf_op jit(solution)/shard_map/ppermute | solution.py:437
  427.9 15.0 %collective-permute-start.9 = (bf16[256,1024]{1,0:T(8,128)(2,1)}, bf16[256,1024]{1,0:T(8,128)(2,1)S(1)}, u32[]{:S(2)}, u32[]{:S(2)}) collective-permute-start(bf16[256,1024]{1,0:T(8,128)(2,1)} %get-tuple-element.47.refs_12_), channel_id=1, source_target_pairs={{2,0},{3,1},{4,2},{5,3},{6,4},{7,5},{14,6},{15,7},{12,14},{13,15},... | collective-permute-start | bytes 1572872 | tf_op jit(solution)/shard_map/ppermute | solution.py:437
  428.4 34.9 %collective-permute-start.3 = (bf16[2,64,4096]{2,1,0:T(8,128)(2,1)}, bf16[2,64,4096]{2,1,0:T(8,128)(2,1)S(1)}, u32[]{:S(2)}, u32[]{:S(2)}) collective-permute-start(bf16[2,64,4096]{2,1,0:T(8,128)(2,1)} %get-tuple-element.45.refs_4_), channel_id=1, source_target_pairs={{2,0},{3,1},{4,2},{5,3},{6,4},{7,5},{14,6},{15,7},{12,14},{13,15},... | collective-permute-start | bytes 3145736 | tf_op jit(solution)/shard_map/ppermute | solution.py:437
  429.8 13.1 %collective-permute-start.6 = (bf16[256,1024]{1,0:T(8,128)(2,1)}, bf16[256,1024]{1,0:T(8,128)(2,1)S(1)}, u32[]{:S(2)}, u32[]{:S(2)}) collective-permute-start(bf16[256,1024]{1,0:T(8,128)(2,1)} %get-tuple-element.46.refs_11_), channel_id=1, source_target_pairs={{0,1},{1,0},{2,3},{3,2},{4,5},{5,4},{6,7},{7,6},{8,9},{9,8},{10,11... | collective-permute-start | bytes 1572872 | tf_op jit(solution)/shard_map/ppermute | solution.py:437
  440.7 3.5 collective-permute-start.7
  442.9 25.8 %collective-permute-start = (bf16[2,64,4096]{2,1,0:T(8,128)(2,1)}, bf16[2,64,4096]{2,1,0:T(8,128)(2,1)S(1)}, u32[]{:S(2)}, u32[]{:S(2)}) collective-permute-start(bf16[2,64,4096]{2,1,0:T(8,128)(2,1)} %get-tuple-element.44.refs_3_), channel_id=1, source_target_pairs={{0,1},{1,0},{2,3},{3,2},{4,5},{5,4},{6,7},{7,6},{8,9},{9,8},{10,11... | collective-permute-start | bytes 3145736 | tf_op jit(solution)/shard_map/ppermute | solution.py:437
  443.7 20.5 %collective-permute-start.10 = (bf16[256,1024]{1,0:T(8,128)(2,1)S(1)}, bf16[256,1024]{1,0:T(8,128)(2,1)S(1)}, u32[]{:S(2)}, u32[]{:S(2)}) collective-permute-start(bf16[256,1024]{1,0:T(8,128)(2,1)S(1)} %collective-permute-done.8.refs_15_), channel_id=1, source_target_pairs={{0,1},{1,0},{2,3},{3,2},{4,5},{5,4},{6,7},{7,6},{8,9},{9,8},{10,11... | collective-permute-start | bytes 1572872 | tf_op jit(solution)/shard_map/ppermute | solution.py:437
  445.0 23.7 %collective-permute-start.1 = (bf16[2,64,4096]{2,1,0:T(8,128)(2,1)}, bf16[2,64,4096]{2,1,0:T(8,128)(2,1)S(1)}, u32[]{:S(2)}, u32[]{:S(2)}) collective-permute-start(bf16[2,64,4096]{2,1,0:T(8,128)(2,1)} %get-tuple-element.45.refs_4_), channel_id=1, source_target_pairs={{0,1},{1,0},{2,3},{3,2},{4,5},{5,4},{6,7},{7,6},{8,9},{9,8},{10,11... | collective-permute-start | bytes 3145736 | tf_op jit(solution)/shard_map/ppermute | solution.py:437
  461.7 4.5 collective-permute-start.11
  463.4 37.5 %collective-permute-start.12 = (bf16[2,64,4096]{2,1,0:T(8,128)(2,1)S(1)}, bf16[2,64,4096]{2,1,0:T(8,128)(2,1)S(1)}, u32[]{:S(2)}, u32[]{:S(2)}) collective-permute-start(bf16[2,64,4096]{2,1,0:T(8,128)(2,1)S(1)} %collective-permute-done.2.refs_7_), channel_id=1, source_target_pairs={{0,2},{1,3},{2,4},{3,5},{4,6},{5,7},{6,14},{7,15},{14,12},{15,13},... | collective-permute-start | bytes 3145736 | tf_op jit(solution)/shard_map/ppermute | solution.py:437
  465.0 35.8 %collective-permute-start.13 = (bf16[2,64,4096]{2,1,0:T(8,128)(2,1)S(1)}, bf16[2,64,4096]{2,1,0:T(8,128)(2,1)S(1)}, u32[]{:S(2)}, u32[]{:S(2)}) collective-permute-start(bf16[2,64,4096]{2,1,0:T(8,128)(2,1)S(1)} %collective-permute-done.3.refs_8_), channel_id=1, source_target_pairs={{2,0},{3,1},{4,2},{5,3},{6,4},{7,5},{14,6},{15,7},{12,14},{13,15},... | collective-permute-start | bytes 3145736 | tf_op jit(solution)/shard_map/ppermute | solution.py:437
  467.0 31.6 %collective-permute-start.16 = (bf16[256,1024]{1,0:T(8,128)(2,1)S(1)}, bf16[256,1024]{1,0:T(8,128)(2,1)}, u32[]{:S(2)}, u32[]{:S(2)}) collective-permute-start(bf16[256,1024]{1,0:T(8,128)(2,1)S(1)} %collective-permute-done.8.refs_15_), channel_id=1, source_target_pairs={{0,2},{1,3},{2,4},{3,5},{4,6},{5,7},{6,14},{7,15},{14,12},{15,13},... | collective-permute-start | bytes 1572872 | tf_op jit(solution)/shard_map/ppermute | solution.py:437
  468.7 41.9 %collective-permute-start.4 = (bf16[2,64,4096]{2,1,0:T(8,128)(2,1)S(1)}, bf16[2,64,4096]{2,1,0:T(8,128)(2,1)S(1)}, u32[]{:S(2)}, u32[]{:S(2)}) collective-permute-start(bf16[2,64,4096]{2,1,0:T(8,128)(2,1)S(1)} %collective-permute-done.2.refs_7_), channel_id=1, source_target_pairs={{0,1},{1,0},{2,3},{3,2},{4,5},{5,4},{6,7},{7,6},{8,9},{9,8},{10,11... | collective-permute-start | bytes 3145736 | tf_op jit(solution)/shard_map/ppermute | solution.py:437
  468.7 75.6 %collective-permute-start.5 = (bf16[2,64,4096]{2,1,0:T(8,128)(2,1)S(1)}, bf16[2,64,4096]{2,1,0:T(8,128)(2,1)S(1)}, u32[]{:S(2)}, u32[]{:S(2)}) collective-permute-start(bf16[2,64,4096]{2,1,0:T(8,128)(2,1)S(1)} %collective-permute-done.3.refs_8_), channel_id=1, source_target_pairs={{0,1},{1,0},{2,3},{3,2},{4,5},{5,4},{6,7},{7,6},{8,9},{9,8},{10,11... | collective-permute-start | bytes 3145736 | tf_op jit(solution)/shard_map/ppermute | solution.py:437
  498.7 12.0 %collective-permute-start.17 = (bf16[256,1024]{1,0:T(8,128)(2,1)S(1)}, bf16[256,1024]{1,0:T(8,128)(2,1)}, u32[]{:S(2)}, u32[]{:S(2)}) collective-permute-start(bf16[256,1024]{1,0:T(8,128)(2,1)S(1)} %collective-permute-done.9.refs_16_), channel_id=1, source_target_pairs={{2,0},{3,1},{4,2},{5,3},{6,4},{7,5},{14,6},{15,7},{12,14},{13,15},... | collective-permute-start | bytes 1572872 | tf_op jit(solution)/shard_map/ppermute | solution.py:437
  500.9 121.7 %collective-permute-start.14 = (bf16[2,64,4096]{2,1,0:T(8,128)(2,1)S(1)}, bf16[2,64,4096]{2,1,0:T(8,128)(2,1)}, u32[]{:S(2)}, u32[]{:S(2)}) collective-permute-start(bf16[2,64,4096]{2,1,0:T(8,128)(2,1)S(1)} %collective-permute-done.12.refs_2_), channel_id=1, source_target_pairs={{0,1},{1,0},{2,3},{3,2},{4,5},{5,4},{6,7},{7,6},{8,9},{9,8},{10,11... | collective-permute-start | bytes 3145736 | tf_op jit(solution)/shard_map/ppermute | solution.py:437
  500.9 121.7 %collective-permute-start.15 = (bf16[2,64,4096]{2,1,0:T(8,128)(2,1)S(1)}, bf16[2,64,4096]{2,1,0:T(8,128)(2,1)}, u32[]{:S(2)}, u32[]{:S(2)}) collective-permute-start(bf16[2,64,4096]{2,1,0:T(8,128)(2,1)S(1)} %collective-permute-done.13.refs_3_), channel_id=1, source_target_pairs={{0,1},{1,0},{2,3},{3,2},{4,5},{5,4},{6,7},{7,6},{8,9},{9,8},{10,11... | collective-permute-start | bytes 3145736 | tf_op jit(solution)/shard_map/ppermute | solution.py:437
  510.7 47.1 %collective-permute-start.18 = (bf16[256,1024]{1,0:T(8,128)(2,1)}, bf16[256,1024]{1,0:T(8,128)(2,1)}, u32[]{:S(2)}, u32[]{:S(2)}) collective-permute-start(bf16[256,1024]{1,0:T(8,128)(2,1)} %collective-permute-done.16.refs_1_), channel_id=1, source_target_pairs={{0,1},{1,0},{2,3},{3,2},{4,5},{5,4},{6,7},{7,6},{8,9},{9,8},{10,11... | collective-permute-start | bytes 1572872 | tf_op jit(solution)/shard_map/ppermute | solution.py:437
  510.7 47.1 %collective-permute-start.19 = (bf16[256,1024]{1,0:T(8,128)(2,1)}, bf16[256,1024]{1,0:T(8,128)(2,1)}, u32[]{:S(2)}, u32[]{:S(2)}) collective-permute-start(bf16[256,1024]{1,0:T(8,128)(2,1)} %collective-permute-done.17.refs_2_), channel_id=1, source_target_pairs={{0,1},{1,0},{2,3},{3,2},{4,5},{5,4},{6,7},{7,6},{8,9},{9,8},{10,11... | collective-permute-start | bytes 1572872 | tf_op jit(solution)/shard_map/ppermute | solution.py:437
  511.2 15.3 %copy-start.19 = (f32[8,128]{1,0:T(8,128)S(1)}, f32[8,128]{1,0:T(8,128)}, u32[]{:S(2)}) copy-start(f32[8,128]{1,0:T(8,128)} %get-tuple-element.38.refs_0_) | copy-start | bytes 12292
  526.1 18.2 %copy-start = (bf16[2,64,4096]{2,1,0:T(8,128)(2,1)S(1)}, bf16[2,64,4096]{2,1,0:T(8,128)(2,1)}, u32[]{:S(2)}) copy-start(bf16[2,64,4096]{2,1,0:T(8,128)(2,1)} %get-tuple-element.44.refs_3_) | copy-start | bytes 3145732
  526.1 18.2 %copy-start.1 = (bf16[2,64,4096]{2,1,0:T(8,128)(2,1)S(1)}, bf16[2,64,4096]{2,1,0:T(8,128)(2,1)}, u32[]{:S(2)}) copy-start(bf16[2,64,4096]{2,1,0:T(8,128)(2,1)} %get-tuple-element.45.refs_4_) | copy-start | bytes 3145732
  526.1 18.2 %copy-start.5 = (bf16[256,1024]{1,0:T(8,128)(2,1)S(1)}, bf16[256,1024]{1,0:T(8,128)(2,1)}, u32[]{:S(2)}) copy-start(bf16[256,1024]{1,0:T(8,128)(2,1)} %get-tuple-element.46.refs_11_) | copy-start | bytes 1572868
  (16 other events, 57.4 us)

commit v4 on v3

--- a/solution.py
+++ b/solution.py
@@ -11,7 +11,8 @@
 BF16 = jnp.bfloat16
 CHIPS = 8
 LAST = 5
-CHUNKS = [(d, w) for w in range(3) for d in range(2)]
+BLOCKS = [(d, w) for w in range(3) for d in range(2)]
+CHUNKS = [(d, w, j) for w in range(3) for j in range(2) for d in range(2)]
 
 
 def device_at(q, c):
@@ -38,7 +39,7 @@
     factor_ref = refs[18]
     edge_gu, edge_dn = refs[19:21], refs[21:23]
     (p_gu, p_dn, r_gu, r_dn, o_gu, o_dn, w_gu, w_dn, m_gu, m_dn, v_gu, v_dn, acc, norms) = refs[23:37]
-    (p_send, p_recv, r_send, r_recv, o_sem, state_sem, a_send, a_recv, n_send, n_recv, l_sem, g_sem) = refs[37:]
+    (p_send, p_first, p_recv, r_send, r_recv, o_sem, state_sem, a_send, s_send, s_recv, n_send, n_recv, l_sem, g_sem) = refs[37:]
 
     rep, dp = lax.axis_index("rep"), lax.axis_index("dp")
     y, z, c = dp // 8, (dp // 2) % 4, dp % 2
@@ -46,12 +47,21 @@
     nxt = [(rep, device_at((q + 1) % CHIPS, c)), (rep, device_at((q + 7) % CHIPS, c))]
     partner = (rep, dp + 1 - 2 * c)
 
-    def pick(gu, dn, lead, d, w):
-        return gu.at[(*lead, d, w)] if w < 2 else dn.at[(*lead, d)]
-
-    def rows_of(array, w, d, dev, lead=()):
+    def half(w, j, start=0):
+        n = 32 if w < 2 else 128
+        if j is None:
+            return pl.ds(start, 2 * n)
+        return pl.ds(start + j * n, n)
+
+    def pick(gu, dn, lead, d, w, j=None):
+        return gu.at[(*lead, d, w, half(w, j))] if w < 2 else dn.at[(*lead, d, half(w, j))]
+
+    def rows_of(array, w, d, dev, lead=(), j=None):
         n = 64 if w < 2 else 256
-        return array[w].at[(*lead, d, pl.ds(pl.multiple_of(dev * n, n), n), slice(None))]
+        return array[w].at[(*lead, d, half(w, j, pl.multiple_of(dev * n, n)), slice(None))]
+
+    def flag(d, w, j):
+        return (d * 3 + w) * 2 + j
 
     def scattered(s, d):
         return (q + 7 - s + CHIPS) % CHIPS if d == 0 else (q + 1 + s) % CHIPS
@@ -59,76 +69,85 @@
     def gathered(h, d):
         return (q + CHIPS - h) % CHIPS if d == 0 else (q + h) % CHIPS
 
+    def whole(gu, dn, sem, *lead):
+        for i, part in enumerate((gu, dn)):
+            ref = part.at[lead] if lead else part
+            pltpu.make_async_copy(ref, ref, sem.at[i]).wait()
+
     def own_load(s, d, w):
         return pltpu.make_async_copy(
-            rows_of(g, w, d, device_at(scattered(s, d), c), (0,)), pick(o_gu, o_dn, (s % 2,), d, w), o_sem.at[s % 2, d * 3 + w]
-        )
-
-    def to_partner(s, d, w):
+            rows_of(g, w, d, device_at(scattered(s, d), c), (0,)), pick(o_gu, o_dn, (s % 2,), d, w), o_sem.at[s % 2, w // 2]
+        )
+
+    def to_partner(s, d, w, j):
         return pltpu.make_async_remote_copy(
-            rows_of(g, w, d, device_at(scattered(s, d), 1 - c), (0,)),
-            pick(p_gu, p_dn, (s,), d, w),
-            p_send.at[s, d * 3 + w],
-            p_recv.at[s, d * 3 + w],
+            rows_of(g, w, d, device_at(scattered(s, d), 1 - c), (0,), j),
+            pick(p_gu, p_dn, (s,), d, w, j),
+            p_send.at[w // 2],
+            p_first.at[flag(d, w, j)] if isinstance(s, int) and s == 0 else p_recv.at[s, w // 2],
             device_id=partner,
             device_id_type=MESH,
         )
 
-    def hop(s, d, w):
+    def hop(s, d, w, j):
         return pltpu.make_async_remote_copy(
-            pick(p_gu, p_dn, (s,), d, w),
-            pick(r_gu, r_dn, (s % 3,), d, w),
-            r_send.at[s % 3, d * 3 + w],
-            r_recv.at[s % 3, d * 3 + w],
+            pick(p_gu, p_dn, (s,), d, w, j),
+            pick(r_gu, r_dn, (s % 3,), d, w, j),
+            r_send.at[w // 2],
+            r_recv.at[s % 3, flag(d, w, j)],
             device_id=nxt[d],
             device_id_type=MESH,
         )
 
     def state_loads(d, w):
-        i = d * 3 + w
         return [
-            pltpu.make_async_copy(m[w].at[d], pick(m_gu, m_dn, (), d, w), state_sem.at[0, i]),
-            pltpu.make_async_copy(v[w].at[d], pick(v_gu, v_dn, (), d, w), state_sem.at[1, i]),
-            pltpu.make_async_copy(rows_of(wt, w, d, dp), pick(w_gu, w_dn, (), d, w), state_sem.at[2, i]),
+            pltpu.make_async_copy(m[w].at[d], pick(m_gu, m_dn, (), d, w), state_sem.at[0, w // 2]),
+            pltpu.make_async_copy(v[w].at[d], pick(v_gu, v_dn, (), d, w), state_sem.at[1, w // 2]),
+            pltpu.make_async_copy(rows_of(wt, w, d, dp), pick(w_gu, w_dn, (), d, w), state_sem.at[2, w // 2]),
         ]
+
+    def sum_out(d, w):
+        return pltpu.make_async_copy(pick(p_gu, p_dn, (7,), d, w), gsum[w].at[d], g_sem.at[w // 2])
 
     barrier = pltpu.get_barrier_semaphore()
     for dev in (*nxt, partner):
         pl.semaphore_signal(barrier, inc=1, device_id=dev, device_id_type=MESH)
-    for d, w in CHUNKS:
+    for d, w in BLOCKS:
         own_load(0, d, w).start()
     pl.semaphore_wait(barrier, 3)
     for s in (0, 1):
-        for d, w in CHUNKS:
-            to_partner(s, d, w).start()
+        for d, w, j in CHUNKS:
+            to_partner(s, d, w, j).start()
 
     def scatter_step(s, first, last):
         if not last:
-            for d, w in CHUNKS:
+            for d, w in BLOCKS:
                 own_load(s + 1, d, w).start()
             if first:
-                for d, w in CHUNKS:
-                    to_partner(s + 2, d, w).start()
+                for d, w, j in CHUNKS:
+                    to_partner(s + 2, d, w, j).start()
             else:
 
                 @pl.when(s < 6)
                 def _():
-                    for d, w in CHUNKS:
-                        to_partner(s + 2, d, w).start()
-
-        for d, w in CHUNKS:
-            own, theirs = pick(o_gu, o_dn, (s % 2,), d, w), pick(p_gu, p_dn, (s,), d, w)
-            own_load(s, d, w).wait()
-            to_partner(s, d, w).wait()
+                    for d, w, j in CHUNKS:
+                        to_partner(s + 2, d, w, j).start()
+
+        whole(o_gu, o_dn, o_sem.at[s % 2], s % 2)
+        if not first:
+            whole(p_gu, p_dn, p_recv.at[s], s)
+        for d, w, j in CHUNKS:
+            own, theirs = pick(o_gu, o_dn, (s % 2,), d, w, j), pick(p_gu, p_dn, (s,), d, w, j)
             if first:
+                to_partner(s, d, w, j).wait_recv()
 
                 def add(rows, cols):
                     theirs[rows, cols] = (own[rows, cols].astype(F32) + theirs[rows, cols].astype(F32)).astype(BF16)
 
             else:
                 before = (s + 2) % 3
-                so_far = pick(r_gu, r_dn, (before,), d, w)
-                hop(s - 1, d, w).wait_recv()
+                so_far = pick(r_gu, r_dn, (before,), d, w, j)
+                hop(s - 1, d, w, j).wait_recv()
 
                 def add(rows, cols):
                     total = (own[rows, cols].astype(F32) + theirs[rows, cols].astype(F32)) + so_far[rows, cols].astype(F32)
@@ -139,18 +158,13 @@
 
             tiles(theirs, add)
             if last:
-                pltpu.make_async_copy(theirs, gsum[w].at[d], g_sem.at[d * 3 + w]).start()
+                if j == 1:
+                    sum_out(d, w).start()
             else:
-                if not first:
-
-                    @pl.when(s >= 3)
-                    def _():
-                        hop(s - 3, d, w).wait_send()
-
-                hop(s, d, w).start()
+                hop(s, d, w, j).start()
 
     scatter_step(0, True, False)
-    for d, w in CHUNKS:
+    for d, w in BLOCKS:
         for copy in state_loads(d, w):
             copy.start()
     acc[...] = jnp.zeros_like(acc)
@@ -161,29 +175,18 @@
     for k in range(1, 8):
         at = pl.ds(k * 128, 128)
         mine += acc[0:8, at] + acc[8:16, at]
-    norms[dp] = mine
-
-    def norm_to(r):
-        return pltpu.make_async_remote_copy(
-            norms.at[dp], norms.at[dp], n_send.at[r], n_recv.at[dp], device_id=(rep, (dp + r) % 16), device_id_type=MESH
-        )
-
-    def norm_from(r):
-        src = (dp + 16 - r) % 16
-        return pltpu.make_async_remote_copy(
-            norms.at[src], norms.at[src], n_send.at[r], n_recv.at[src], device_id=(rep, src), device_id_type=MESH
-        )
-
+    norms[dp] = jnp.sum(mine, axis=0, keepdims=True)
     for r in range(1, 16):
-        norm_to(r).start()
-    for s in (4, 5, 6):
-        for d, w in CHUNKS:
-            hop(s, d, w).wait_send()
-    for d, w in CHUNKS:
-        for copy in state_loads(d, w):
-            copy.wait()
-    for r in range(1, 16):
-        norm_from(r).wait_recv()
+        pltpu.make_async_remote_copy(
+            norms.at[dp], norms.at[dp], n_send.at[0], n_recv.at[0], device_id=(rep, (dp + r) % 16), device_id_type=MESH
+        ).start()
+    whole(p_gu, p_dn, r_send, pl.ds(0, 7))
+    whole(p_gu, p_dn, p_send)
+    for i, (gu, dn) in enumerate(((m_gu, m_dn), (v_gu, v_dn), (w_gu, w_dn))):
+        whole(gu, dn, state_sem.at[i])
+    others = norms.at[pl.ds(0, 15)]
+    pltpu.make_async_copy(others, others, n_send.at[0]).wait()
+    pltpu.make_async_copy(others, others, n_recv.at[0]).wait()
     squares = norms[0]
     for k in range(1, 16):
         squares += norms[k]
@@ -193,50 +196,44 @@
     factor_ref[...] = factor
     scale = jnp.broadcast_to(factor[0:1, 0:1], (16, 1024))
 
-    def edge(d, w):
-        return edge_gu[d].at[w] if w < 2 else edge_dn[d]
-
-    def held(h, d, w):
+    def edge(d, w, j):
+        return edge_gu[d].at[w, half(w, j)] if w < 2 else edge_dn[d].at[half(w, j)]
+
+    def held(h, d, w, j):
         if isinstance(h, int) and h == 0:
-            return pick(p_gu, p_dn, (0,), d, w)
+            return pick(p_gu, p_dn, (0,), d, w, j)
         if isinstance(h, int) and h == LAST:
-            return edge(d, w)
-        return rows_of(x, w, d, device_at(gathered(h, d), c))
-
-    def gather_hop(h, d, w):
-        dst = edge(d, w) if isinstance(h, int) and h == LAST - 1 else rows_of(x, w, d, device_at(gathered(h, d), c))
+            return edge(d, w, j)
+        return rows_of(x, w, d, device_at(gathered(h, d), c), (), j)
+
+    def gather_hop(h, d, w, j):
+        dst = edge(d, w, j) if isinstance(h, int) and h == LAST - 1 else rows_of(x, w, d, device_at(gathered(h, d), c), (), j)
         return pltpu.make_async_remote_copy(
-            held(h, d, w), dst, a_send.at[h, d * 3 + w], a_recv.at[h, d * 3 + w], device_id=nxt[d], device_id_type=MESH
-        )
-
-    def gather_from(h, d, w):
-        block = held(h, d, w)
+            held(h, d, w, j), dst, a_send.at[w // 2], r_recv.at[(h + 1) % 3, flag(d, w, j)], device_id=nxt[d], device_id_type=MESH
+        )
+
+    def gather_from(h, d, w, j):
+        block = held(h, d, w, j)
         return pltpu.make_async_remote_copy(
-            block, block, a_send.at[h - 1, d * 3 + w], a_recv.at[h - 1, d * 3 + w], device_id=nxt[d], device_id_type=MESH
-        )
-
-    def share(h, d, w):
+            block, block, a_send.at[w // 2], r_recv.at[h % 3, flag(d, w, j)], device_id=nxt[d], device_id_type=MESH
+        )
+
+    def share(h, d, w, j):
         return pltpu.make_async_remote_copy(
-            held(h, d, w),
-            rows_of(x, w, d, device_at(gathered(h, d), c)),
-            p_send.at[h, d * 3 + w],
-            p_recv.at[h, d * 3 + w],
+            held(h, d, w, j),
+            rows_of(x, w, d, device_at(gathered(h, d), c), (), j),
+            s_send.at[w // 2],
+            s_recv.at[w // 2],
             device_id=partner,
             device_id_type=MESH,
         )
 
-    def shared(h, d, w):
-        block = rows_of(x, w, d, device_at(gathered(h, d), 1 - c))
-        return pltpu.make_async_remote_copy(
-            block, block, p_send.at[h, d * 3 + w], p_recv.at[h, d * 3 + w], device_id=partner, device_id_type=MESH
-        )
-
     def keep(d, w):
-        return pltpu.make_async_copy(pick(p_gu, p_dn, (0,), d, w), rows_of(x, w, d, dp), l_sem.at[d * 3 + w])
-
-    for d, w in CHUNKS:
-        gr, new = pick(p_gu, p_dn, (7,), d, w), pick(p_gu, p_dn, (0,), d, w)
-        mr, vr, wr = pick(m_gu, m_dn, (), d, w), pick(v_gu, v_dn, (), d, w), pick(w_gu, w_dn, (), d, w)
+        return pltpu.make_async_copy(pick(p_gu, p_dn, (0,), d, w), rows_of(x, w, d, dp), l_sem.at[w // 2])
+
+    for d, w, j in CHUNKS:
+        gr, new = pick(p_gu, p_dn, (7,), d, w, j), pick(p_gu, p_dn, (0,), d, w, j)
+        mr, vr, wr = pick(m_gu, m_dn, (), d, w, j), pick(v_gu, v_dn, (), d, w, j), pick(w_gu, w_dn, (), d, w, j)
 
         def update(rows, cols):
             grad = gr[rows, cols].astype(F32) * scale
@@ -246,41 +243,27 @@
             new[rows, cols] = (old - 0.02 * (m1 * lax.rsqrt(v1 + 1e-8) + 0.1 * old)).astype(BF16)
 
         tiles(new, update)
-        gather_hop(0, d, w).start()
-        share(0, d, w).start()
-        keep(d, w).start()
+        gather_hop(0, d, w, j).start()
+        share(0, d, w, j).start()
+        if j == 1:
+            keep(d, w).start()
 
     def gather_step(h, carry):
-        for d, w in CHUNKS:
-            gather_from(h, d, w).wait_recv()
-            gather_hop(h, d, w).start()
-            share(h, d, w).start()
+        for d, w, j in CHUNKS:
+            gather_from(h, d, w, j).wait_recv()
+            gather_hop(h, d, w, j).start()
+            share(h, d, w, j).start()
         return carry
 
     lax.fori_loop(1, LAST - 1, gather_step, 0)
     gather_step(LAST - 1, 0)
-    for d, w in CHUNKS:
-        gather_from(LAST, d, w).wait_recv()
-
-    for r in range(1, 16):
-        norm_to(r).wait_send()
-    for d, w in CHUNKS:
-        keep(d, w).wait()
-        pltpu.make_async_copy(pick(p_gu, p_dn, (7,), d, w), gsum[w].at[d], g_sem.at[d * 3 + w]).wait()
-
-    def drain(h, carry):
-        for d, w in CHUNKS:
-            gather_from(h + 1, d, w).wait_send()
-        return carry
-
-    lax.fori_loop(0, LAST, drain, 0)
-
-    def drain_shares(h, carry):
-        for d, w in CHUNKS:
-            shared(h, d, w).wait()
-        return carry
-
-    lax.fori_loop(0, LAST, drain_shares, 0)
+    whole(p_gu, p_dn, l_sem, 0)
+    whole(p_gu, p_dn, g_sem, 7)
+    whole(p_gu, p_dn, s_send, pl.ds(0, LAST))
+    whole(p_gu, p_dn, s_recv, pl.ds(0, LAST))
+    for d, w, j in CHUNKS:
+        gather_from(LAST, d, w, j).wait_recv()
+    whole(p_gu, p_dn, a_send, pl.ds(0, LAST))
 
 
 def place():
@@ -362,11 +345,11 @@
             pltpu.make_async_copy(pick(v_gu, v_dn, d, w), v_out[w].at[d], state_out.at[1, i]),
         ]
 
-    for d, w in CHUNKS:
+    for d, w in BLOCKS:
         for one in load(d, w):
             one.start()
     scale = jnp.broadcast_to(factor[0:1, 0:1], (16, 1024))
-    for d, w in CHUNKS:
+    for d, w in BLOCKS:
         for one in load(d, w):
             one.wait()
         gr, mr, vr = pick(g_gu, g_dn, d, w), pick(m_gu, m_dn, d, w), pick(v_gu, v_dn, d, w)
@@ -380,7 +363,7 @@
         for one in store(d, w):
             one.start()
     through(arrived(x, out), slots, in_sem, out_sem)
-    for d, w in CHUNKS:
+    for d, w in BLOCKS:
         for one in store(d, w):
             one.wait()
 
@@ -462,9 +445,9 @@
                 *pair((), F32),
                 *pair((), F32),
                 pltpu.VMEM((16, 1024), F32),
-                pltpu.VMEM((16, 8, 128), F32),
-                dma((8, 6)), dma((8, 6)), dma((3, 6)), dma((3, 6)), dma((2, 6)), dma((3, 6)),
-                dma((7, 6)), dma((7, 6)), dma((16,)), dma((16,)), dma((6,)), dma((6,)),
+                pltpu.VMEM((16, 1, 128), F32),
+                dma((2,)), dma((12,)), dma((8, 2)), dma((2,)), dma((3, 12)), dma((2, 2)), dma((3, 2)),
+                dma((2,)), dma((2,)), dma((2,)), dma((1,)), dma((1,)), dma((2,)), dma((2,)),
             ],
             compiler_params=pltpu.CompilerParams(collective_id=0, has_side_effects=True, vmem_limit_bytes=66 * 1000 * 1000),
             name="step",

time: 688 us -> 683 us (level)
  no operation moved by 1% of the time
where the time goes in v4:
time: 683 us
  Pallas kernels  589 us (86%)
  waiting for transfers between devices  70.5 us (10%)
  local copies, waits for them, and re-layouts  12.6 us (2%)
  starting transfers between devices  10.2 us (1%)
    pallas_call x1, Pallas kernels, step(): pl.pallas_call(kernel, out_shape=[*shapes(whole + block, BF16), jax.Shape...  421 us
    pallas_call x5, Pallas kernels, call_local(): pl.pallas_call(body, out_shape=outs, in_specs=specs or [hbm] * len(ins),...  168 us
    ppermute x20, waiting for transfers between devices, permute(): return lax.ppermute(array, 'dp', pairs)  70.5 us
  transfers between devices with their start and end apart: 20, of which 6 were waited for; matrix products, arithmetic and copies ran while one was open for 0% of the time, Pallas kernels for 15%

profile of v4, /device:TPU:0, one launch (start us, length us, event | category | flops | bytes accessed | tf_op | source)
XLA Modules:
  0.0 683.0 jit_solution(8721782677040833545)
XLA Ops:
  0.6 420.6 %step.1 = (bf16[2,1024,4096]{2,1,0:T(8,128)(2,1)}, bf16[2,1024,4096]{2,1,0:T(8,128)(2,1)}, bf16[2,4096,1024]{2,1,0:T(8,128)(2,1)}, bf16[2,64,4096]{2,1,0:T(8,128...) custom-call(bf16[1,2,1024,4096]{3,2,1,0:T(8,128)(2,1)} %refs_0_.1, ...), custom_call_target="tpu_custom_call" | custom-call | tf_op jit(solution)/shard_map/step/pallas_call | solution.py:431
  421.2 1.0 collective-permute-start.8
  423.0 1.2 collective-permute-start.9
  424.3 1.0 collective-permute-start.3
  425.3 10.9 %collective-permute-done.8.refs_15_ = bf16[256,1024]{1,0:T(8,128)(2,1)S(1)} collective-permute-done((bf16[256,1024]{1,0:T(8,128)(2,1)}, bf16[256,1024]{1,0:T(8,128)(2,1)S(1)}, u32[]{:S(2)}, u32[]{:S(2)}) %collective-permute-start.8) | collective-permute-done | bytes 524320 | tf_op jit(solution)/shard_map/ppermute | solution.py:420
  436.3 1.8 collective-permute-done.9.refs_16_
  440.2 16.8 %collective-permute-done.2.refs_7_ = bf16[2,64,4096]{2,1,0:T(8,128)(2,1)S(1)} collective-permute-done((bf16[2,64,4096]{2,1,0:T(8,128)(2,1)}, bf16[2,64,4096]{2,1,0:T(8,128)(2,1)S(1)}, u32[]{:S(2)}, u32[]{:S(2)}) %collective-permute-start.2) | collective-permute-done | bytes 1048608 | tf_op jit(solution)/shard_map/ppermute | solution.py:420
  457.0 1.2 collective-permute-done.3.refs_8_
  459.8 1.3 collective-permute-start.13
  464.0 30.0 %collective-permute-done.16.refs_1_ = bf16[256,1024]{1,0:T(8,128)(2,1)} collective-permute-done((bf16[256,1024]{1,0:T(8,128)(2,1)S(1)}, bf16[256,1024]{1,0:T(8,128)(2,1)}, u32[]{:S(2)}, u32[]{:S(2)}) %collective-permute-start.16) | collective-permute-done | bytes 524320 | tf_op jit(solution)/shard_map/ppermute | solution.py:420
  493.9 1.3 collective-permute-start.17
  496.6 9.7 %collective-permute-done.17.refs_2_ = bf16[256,1024]{1,0:T(8,128)(2,1)} collective-permute-done((bf16[256,1024]{1,0:T(8,128)(2,1)S(1)}, bf16[256,1024]{1,0:T(8,128)(2,1)}, u32[]{:S(2)}, u32[]{:S(2)}) %collective-permute-start.17) | collective-permute-done | bytes 524320 | tf_op jit(solution)/shard_map/ppermute | solution.py:420
  506.8 14.9 %shard_map.187 = (bf16[2,1024,4096]{2,1,0:T(8,128)(2,1)}, bf16[2,1024,4096]{2,1,0:T(8,128)(2,1)}) custom-call(bf16[2,1024,4096]{2,1,0:T(8,128)(2,1)} %get-tuple-element.34.xg, bf16[2,1024,4096]{2,1,0:T(8,128)(2,1)} %get-tuple-element.35.xu), custom_call_target="tpu_custom_call" | custom-call | flops 1677721600 | bytes 41943040 | tf_op jit(solution)/shard_map/pallas_call | solution.py:408
  522.1 17.8 %shard_map.188 = (bf16[2,4096,1024]{2,1,0:T(8,128)(2,1)}, f32[2,64,4096]{2,1,0:T(8,128)}, f32[2,64,4096]{2,1,0:T(8,128)}, f32[2,256,1024]{2,1,0:T(8,128)}, f32[2...) custom-call(f32[8,128]{1,0:T(8,128)S(1)} %copy-done.19, ...), custom_call_target="tpu_custom_call" | custom-call | flops 2013265920 | bytes 50331648 | tf_op jit(solution)/shard_map/pallas_call | solution.py:408
  540.0 1.0 copy-done.6
  541.0 1.0 copy-done.8
  542.1 1.0 copy-done.10
  543.1 1.0 copy-done.12
  544.2 1.0 copy-done.14
  545.2 1.0 copy-done.16
  546.3 1.0 copy-done.18
  547.3 6.1 shard_map.189
  553.5 64.7 %shard_map.191 = bf16[2,4096,1024]{2,1,0:T(8,128)(2,1)} custom-call(bf16[2,4096,1024]{2,1,0:T(8,128)(2,1)} %get-tuple-element.52.refs_0_, bf16[256,1024]{1,0:T(8,128)(2,1)} %collective-permute-done.16.refs_1_, bf16[256,1024]{1,0:T(8,128)(2,1)} %collective-permute-done.17.refs_2_, ...), custom_call_target="tpu_custom_call", output_to_operand_aliasing={{}: (0, {})} | custom-call | flops 167772160 | bytes 4194304 | tf_op jit(solution)/shard_map/pallas_call | solution.py:408
  618.2 64.8 %shard_map.190 = (bf16[2,1024,4096]{2,1,0:T(8,128)(2,1)}, bf16[2,1024,4096]{2,1,0:T(8,128)(2,1)}) custom-call(bf16[2,1024,4096]{2,1,0:T(8,128)(2,1)} %get-tuple-element.48.refs_0_, bf16[2,1024,4096]{2,1,0:T(8,128)(2,1)} %get-tuple-element.49.refs_1_, ...), custom_call_target="tpu_custom_call", output_to_operand_aliasing={{0}: (0, {}), {1}: (1, {})} | custom-call | flops 335544320 | bytes 8388608 | tf_op jit(solution)/shard_map/pallas_call | solution.py:408
  (62 shorter events, 9.6 us)
Async XLA Ops:
  421.2 15.1 %collective-permute-start.8 = (bf16[256,1024]{1,0:T(8,128)(2,1)}, bf16[256,1024]{1,0:T(8,128)(2,1)S(1)}, u32[]{:S(2)}, u32[]{:S(2)}) collective-permute-start(bf16[256,1024]{1,0:T(8,128)(2,1)} %get-tuple-element.46.refs_11_), channel_id=1, source_target_pairs={{0,2},{1,3},{2,4},{3,5},{4,6},{5,7},{6,14},{7,15},{14,12},{15,13},... | collective-permute-start | bytes 1572872 | tf_op jit(solution)/shard_map/ppermute | solution.py:420
  422.2 34.8 %collective-permute-start.2 = (bf16[2,64,4096]{2,1,0:T(8,128)(2,1)}, bf16[2,64,4096]{2,1,0:T(8,128)(2,1)S(1)}, u32[]{:S(2)}, u32[]{:S(2)}) collective-permute-start(bf16[2,64,4096]{2,1,0:T(8,128)(2,1)} %get-tuple-element.44.refs_3_), channel_id=1, source_target_pairs={{0,2},{1,3},{2,4},{3,5},{4,6},{5,7},{6,14},{7,15},{14,12},{15,13},... | collective-permute-start | bytes 3145736 | tf_op jit(solution)/shard_map/ppermute | solution.py:420
  423.0 15.0 %collective-permute-start.9 = (bf16[256,1024]{1,0:T(8,128)(2,1)}, bf16[256,1024]{1,0:T(8,128)(2,1)S(1)}, u32[]{:S(2)}, u32[]{:S(2)}) collective-permute-start(bf16[256,1024]{1,0:T(8,128)(2,1)} %get-tuple-element.47.refs_12_), channel_id=1, source_target_pairs={{2,0},{3,1},{4,2},{5,3},{6,4},{7,5},{14,6},{15,7},{12,14},{13,15},... | collective-permute-start | bytes 1572872 | tf_op jit(solution)/shard_map/ppermute | solution.py:420
  424.3 34.0 %collective-permute-start.3 = (bf16[2,64,4096]{2,1,0:T(8,128)(2,1)}, bf16[2,64,4096]{2,1,0:T(8,128)(2,1)S(1)}, u32[]{:S(2)}, u32[]{:S(2)}) collective-permute-start(bf16[2,64,4096]{2,1,0:T(8,128)(2,1)} %get-tuple-element.45.refs_4_), channel_id=1, source_target_pairs={{2,0},{3,1},{4,2},{5,3},{6,4},{7,5},{14,6},{15,7},{12,14},{13,15},... | collective-permute-start | bytes 3145736 | tf_op jit(solution)/shard_map/ppermute | solution.py:420
  425.3 12.7 %collective-permute-start.6 = (bf16[256,1024]{1,0:T(8,128)(2,1)}, bf16[256,1024]{1,0:T(8,128)(2,1)S(1)}, u32[]{:S(2)}, u32[]{:S(2)}) collective-permute-start(bf16[256,1024]{1,0:T(8,128)(2,1)} %get-tuple-element.46.refs_11_), channel_id=1, source_target_pairs={{0,1},{1,0},{2,3},{3,2},{4,5},{5,4},{6,7},{7,6},{8,9},{9,8},{10,11... | collective-permute-start | bytes 1572872 | tf_op jit(solution)/shard_map/ppermute | solution.py:420
  436.3 3.1 collective-permute-start.7
  438.0 25.4 %collective-permute-start = (bf16[2,64,4096]{2,1,0:T(8,128)(2,1)}, bf16[2,64,4096]{2,1,0:T(8,128)(2,1)S(1)}, u32[]{:S(2)}, u32[]{:S(2)}) collective-permute-start(bf16[2,64,4096]{2,1,0:T(8,128)(2,1)} %get-tuple-element.44.refs_3_), channel_id=1, source_target_pairs={{0,1},{1,0},{2,3},{3,2},{4,5},{5,4},{6,7},{7,6},{8,9},{9,8},{10,11... | collective-permute-start | bytes 3145736 | tf_op jit(solution)/shard_map/ppermute | solution.py:420
  438.9 20.1 %collective-permute-start.10 = (bf16[256,1024]{1,0:T(8,128)(2,1)S(1)}, bf16[256,1024]{1,0:T(8,128)(2,1)S(1)}, u32[]{:S(2)}, u32[]{:S(2)}) collective-permute-start(bf16[256,1024]{1,0:T(8,128)(2,1)S(1)} %collective-permute-done.8.refs_15_), channel_id=1, source_target_pairs={{0,1},{1,0},{2,3},{3,2},{4,5},{5,4},{6,7},{7,6},{8,9},{9,8},{10,11... | collective-permute-start | bytes 1572872 | tf_op jit(solution)/shard_map/ppermute | solution.py:420
  440.2 23.3 %collective-permute-start.1 = (bf16[2,64,4096]{2,1,0:T(8,128)(2,1)}, bf16[2,64,4096]{2,1,0:T(8,128)(2,1)S(1)}, u32[]{:S(2)}, u32[]{:S(2)}) collective-permute-start(bf16[2,64,4096]{2,1,0:T(8,128)(2,1)} %get-tuple-element.45.refs_4_), channel_id=1, source_target_pairs={{0,1},{1,0},{2,3},{3,2},{4,5},{5,4},{6,7},{7,6},{8,9},{9,8},{10,11... | collective-permute-start | bytes 3145736 | tf_op jit(solution)/shard_map/ppermute | solution.py:420
  457.0 4.1 collective-permute-start.11
  458.2 37.8 %collective-permute-start.12 = (bf16[2,64,4096]{2,1,0:T(8,128)(2,1)S(1)}, bf16[2,64,4096]{2,1,0:T(8,128)(2,1)S(1)}, u32[]{:S(2)}, u32[]{:S(2)}) collective-permute-start(bf16[2,64,4096]{2,1,0:T(8,128)(2,1)S(1)} %collective-permute-done.2.refs_7_), channel_id=1, source_target_pairs={{0,2},{1,3},{2,4},{3,5},{4,6},{5,7},{6,14},{7,15},{14,12},{15,13},... | collective-permute-start | bytes 3145736 | tf_op jit(solution)/shard_map/ppermute | solution.py:420
  459.8 36.3 %collective-permute-start.13 = (bf16[2,64,4096]{2,1,0:T(8,128)(2,1)S(1)}, bf16[2,64,4096]{2,1,0:T(8,128)(2,1)S(1)}, u32[]{:S(2)}, u32[]{:S(2)}) collective-permute-start(bf16[2,64,4096]{2,1,0:T(8,128)(2,1)S(1)} %collective-permute-done.3.refs_8_), channel_id=1, source_target_pairs={{2,0},{3,1},{4,2},{5,3},{6,4},{7,5},{14,6},{15,7},{12,14},{13,15},... | collective-permute-start | bytes 3145736 | tf_op jit(solution)/shard_map/ppermute | solution.py:420
  461.9 32.0 %collective-permute-start.16 = (bf16[256,1024]{1,0:T(8,128)(2,1)S(1)}, bf16[256,1024]{1,0:T(8,128)(2,1)}, u32[]{:S(2)}, u32[]{:S(2)}) collective-permute-start(bf16[256,1024]{1,0:T(8,128)(2,1)S(1)} %collective-permute-done.8.refs_15_), channel_id=1, source_target_pairs={{0,2},{1,3},{2,4},{3,5},{4,6},{5,7},{6,14},{7,15},{14,12},{15,13},... | collective-permute-start | bytes 1572872 | tf_op jit(solution)/shard_map/ppermute | solution.py:420
  463.5 42.8 %collective-permute-start.4 = (bf16[2,64,4096]{2,1,0:T(8,128)(2,1)S(1)}, bf16[2,64,4096]{2,1,0:T(8,128)(2,1)S(1)}, u32[]{:S(2)}, u32[]{:S(2)}) collective-permute-start(bf16[2,64,4096]{2,1,0:T(8,128)(2,1)S(1)} %collective-permute-done.2.refs_7_), channel_id=1, source_target_pairs={{0,1},{1,0},{2,3},{3,2},{4,5},{5,4},{6,7},{7,6},{8,9},{9,8},{10,11... | collective-permute-start | bytes 3145736 | tf_op jit(solution)/shard_map/ppermute | solution.py:420
  463.5 76.5 %collective-permute-start.5 = (bf16[2,64,4096]{2,1,0:T(8,128)(2,1)S(1)}, bf16[2,64,4096]{2,1,0:T(8,128)(2,1)S(1)}, u32[]{:S(2)}, u32[]{:S(2)}) collective-permute-start(bf16[2,64,4096]{2,1,0:T(8,128)(2,1)S(1)} %collective-permute-done.3.refs_8_), channel_id=1, source_target_pairs={{0,1},{1,0},{2,3},{3,2},{4,5},{5,4},{6,7},{7,6},{8,9},{9,8},{10,11... | collective-permute-start | bytes 3145736 | tf_op jit(solution)/shard_map/ppermute | solution.py:420
  493.9 12.4 %collective-permute-start.17 = (bf16[256,1024]{1,0:T(8,128)(2,1)S(1)}, bf16[256,1024]{1,0:T(8,128)(2,1)}, u32[]{:S(2)}, u32[]{:S(2)}) collective-permute-start(bf16[256,1024]{1,0:T(8,128)(2,1)S(1)} %collective-permute-done.9.refs_16_), channel_id=1, source_target_pairs={{2,0},{3,1},{4,2},{5,3},{6,4},{7,5},{14,6},{15,7},{12,14},{13,15},... | collective-permute-start | bytes 1572872 | tf_op jit(solution)/shard_map/ppermute | solution.py:420
  496.1 122.1 %collective-permute-start.14 = (bf16[2,64,4096]{2,1,0:T(8,128)(2,1)S(1)}, bf16[2,64,4096]{2,1,0:T(8,128)(2,1)}, u32[]{:S(2)}, u32[]{:S(2)}) collective-permute-start(bf16[2,64,4096]{2,1,0:T(8,128)(2,1)S(1)} %collective-permute-done.12.refs_2_), channel_id=1, source_target_pairs={{0,1},{1,0},{2,3},{3,2},{4,5},{5,4},{6,7},{7,6},{8,9},{9,8},{10,11... | collective-permute-start | bytes 3145736 | tf_op jit(solution)/shard_map/ppermute | solution.py:420
  496.1 122.1 %collective-permute-start.15 = (bf16[2,64,4096]{2,1,0:T(8,128)(2,1)S(1)}, bf16[2,64,4096]{2,1,0:T(8,128)(2,1)}, u32[]{:S(2)}, u32[]{:S(2)}) collective-permute-start(bf16[2,64,4096]{2,1,0:T(8,128)(2,1)S(1)} %collective-permute-done.13.refs_3_), channel_id=1, source_target_pairs={{0,1},{1,0},{2,3},{3,2},{4,5},{5,4},{6,7},{7,6},{8,9},{9,8},{10,11... | collective-permute-start | bytes 3145736 | tf_op jit(solution)/shard_map/ppermute | solution.py:420
  506.3 47.1 %collective-permute-start.18 = (bf16[256,1024]{1,0:T(8,128)(2,1)}, bf16[256,1024]{1,0:T(8,128)(2,1)}, u32[]{:S(2)}, u32[]{:S(2)}) collective-permute-start(bf16[256,1024]{1,0:T(8,128)(2,1)} %collective-permute-done.16.refs_1_), channel_id=1, source_target_pairs={{0,1},{1,0},{2,3},{3,2},{4,5},{5,4},{6,7},{7,6},{8,9},{9,8},{10,11... | collective-permute-start | bytes 1572872 | tf_op jit(solution)/shard_map/ppermute | solution.py:420
  506.3 47.1 %collective-permute-start.19 = (bf16[256,1024]{1,0:T(8,128)(2,1)}, bf16[256,1024]{1,0:T(8,128)(2,1)}, u32[]{:S(2)}, u32[]{:S(2)}) collective-permute-start(bf16[256,1024]{1,0:T(8,128)(2,1)} %collective-permute-done.17.refs_2_), channel_id=1, source_target_pairs={{0,1},{1,0},{2,3},{3,2},{4,5},{5,4},{6,7},{7,6},{8,9},{9,8},{10,11... | collective-permute-start | bytes 1572872 | tf_op jit(solution)/shard_map/ppermute | solution.py:420
  506.8 15.3 %copy-start.19 = (f32[8,128]{1,0:T(8,128)S(1)}, f32[8,128]{1,0:T(8,128)}, u32[]{:S(2)}) copy-start(f32[8,128]{1,0:T(8,128)} %get-tuple-element.38.refs_0_) | copy-start | bytes 12292
  521.7 18.2 %copy-start = (bf16[2,64,4096]{2,1,0:T(8,128)(2,1)S(1)}, bf16[2,64,4096]{2,1,0:T(8,128)(2,1)}, u32[]{:S(2)}) copy-start(bf16[2,64,4096]{2,1,0:T(8,128)(2,1)} %get-tuple-element.44.refs_3_) | copy-start | bytes 3145732
  521.7 18.2 %copy-start.1 = (bf16[2,64,4096]{2,1,0:T(8,128)(2,1)S(1)}, bf16[2,64,4096]{2,1,0:T(8,128)(2,1)}, u32[]{:S(2)}) copy-start(bf16[2,64,4096]{2,1,0:T(8,128)(2,1)} %get-tuple-element.45.refs_4_) | copy-start | bytes 3145732
  521.7 18.2 %copy-start.5 = (bf16[256,1024]{1,0:T(8,128)(2,1)S(1)}, bf16[256,1024]{1,0:T(8,128)(2,1)}, u32[]{:S(2)}) copy-start(bf16[256,1024]{1,0:T(8,128)(2,1)} %get-tuple-element.46.refs_11_) | copy-start | bytes 1572868
  (16 other events, 57.4 us)

commit v5 on v4

--- a/solution.py
+++ b/solution.py
@@ -39,7 +39,7 @@
     factor_ref = refs[18]
     edge_gu, edge_dn = refs[19:21], refs[21:23]
     (p_gu, p_dn, r_gu, r_dn, o_gu, o_dn, w_gu, w_dn, m_gu, m_dn, v_gu, v_dn, acc, norms) = refs[23:37]
-    (p_send, p_first, p_recv, r_send, r_recv, o_sem, state_sem, a_send, s_send, s_recv, n_send, n_recv, l_sem, g_sem) = refs[37:]
+    (p_send, p_recv, r_send, r_recv, o_sem, state_sem, a_send, s_send, s_recv, n_send, n_recv, l_sem, g_sem) = refs[37:]
 
     rep, dp = lax.axis_index("rep"), lax.axis_index("dp")
     y, z, c = dp // 8, (dp // 2) % 4, dp % 2
@@ -84,7 +84,7 @@
             rows_of(g, w, d, device_at(scattered(s, d), 1 - c), (0,), j),
             pick(p_gu, p_dn, (s,), d, w, j),
             p_send.at[w // 2],
-            p_first.at[flag(d, w, j)] if isinstance(s, int) and s == 0 else p_recv.at[s, w // 2],
+            r_recv.at[2, flag(d, w, j)] if isinstance(s, int) and s == 0 else p_recv.at[s, w // 2],
             device_id=partner,
             device_id_type=MESH,
         )
@@ -287,13 +287,14 @@
     return [(block_rows(x, d, chip, 2), block_rows(out, d, chip, 2)) for d, chip in chips]
 
 
-def landed(hop, lands, outs):
+def landed(hop, lands, outs, first=0, at=None):
     _, q, c = place()
     pairs = []
-    for i, land in enumerate(lands):
+    for i, land in enumerate(lands, first):
         dev = device_at(from_chip(q, hop, i % 2), c if i < 2 else 1 - c)
         for w, out in enumerate(outs):
-            pairs.append((land.at[w] if len(outs) > 1 else land, block_rows(out, i % 2, dev)))
+            target = block_rows(out, i % 2, dev)
+            pairs.append((land.at[w] if len(outs) > 1 else land, target if at is None else target.at[at]))
     return pairs
 
 
@@ -376,13 +377,24 @@
     through(down, down_slots, in_sem, out_sem)
 
 
-def finish(weights, *refs):
-    lands, outs, sem = refs[weights : weights + 4], refs[weights + 4 : 2 * weights + 4], refs[-1]
-    copies = [pltpu.make_async_copy(src, dst, sem.at[i]) for i, (src, dst) in enumerate(landed(LAST + 2, lands, outs))]
+def in_place(pairs, sem):
+    copies = [pltpu.make_async_copy(src, dst, sem.at[i]) for i, (src, dst) in enumerate(pairs)]
     for copy in copies:
         copy.start()
     for copy in copies:
         copy.wait()
+
+
+def finish_wide(*refs):
+    through(landed(LAST + 2, refs[2:6], refs[6:8]), *refs[8:])
+
+
+def finish_deep(*refs):
+    in_place(landed(LAST + 2, refs[1:5], refs[5:6], 0, pl.ds(0, 128)), refs[6])
+
+
+def finish_tail(*refs):
+    in_place(landed(LAST + 2, refs[1:5], refs[5:6], 0, pl.ds(128, 128)), refs[6])
 
 
 def solution(mesh):
@@ -446,7 +458,7 @@
                 *pair((), F32),
                 pltpu.VMEM((16, 1024), F32),
                 pltpu.VMEM((16, 1, 128), F32),
-                dma((2,)), dma((12,)), dma((8, 2)), dma((2,)), dma((3, 12)), dma((2, 2)), dma((3, 2)),
+                dma((2,)), dma((8, 2)), dma((2,)), dma((3, 12)), dma((2, 2)), dma((3, 2)),
                 dma((2,)), dma((2,)), dma((2,)), dma((1,)), dma((1,)), dma((2,)), dma((2,)),
             ],
             compiler_params=pltpu.CompilerParams(collective_id=0, has_side_effects=True, vmem_limit_bytes=66 * 1000 * 1000),
@@ -480,7 +492,8 @@
             50,
             specs=[vmem] + [hbm] * 10,
         )
-        deep7, their_deep6 = hop_on(deep6), cross(deep6)
+        deep7, their_deep6 = hop_on([e[:128] for e in deep6]), cross(deep6)
+        tail7 = hop_on([e[128:] for e in deep6])
         news = local(
             settle,
             shapes(whole, BF16),
@@ -493,13 +506,19 @@
         )
         their_wide7 = cross(wide7)
         new_g, new_u = local(
-            lambda *refs: finish(2, *refs), shapes(whole[:2], BF16), (*news[:2], *wide7, *their_wide7), [dma((8,))],
+            finish_wide, shapes(whole[:2], BF16), (*news[:2], *wide7, *their_wide7),
+            [pltpu.VMEM((16, 64, 4096), BF16), *slots],
             8 * mib, 24, {0: 0, 1: 1}, [hbm] * 2 + [anywhere] * 4,
         )
         their_deep7 = cross(deep7)
+        their_tail7 = cross(tail7)
         (new_d,) = local(
-            lambda *refs: finish(1, *refs), shapes(whole[2:], BF16), (news[2], *deep7, *their_deep7), [dma((8,))],
-            4 * mib, 24, {0: 0}, [hbm] + [anywhere] * 4,
+            finish_deep, shapes(whole[2:], BF16), (news[2], *deep7, *their_deep7), [dma((4,))],
+            2 * mib, 24, {0: 0}, [hbm] + [anywhere] * 4,
+        )
+        (new_d,) = local(
+            finish_tail, shapes(whole[2:], BF16), (new_d, *tail7, *their_tail7), [dma((4,))], 2 * mib, 24,
+            {0: 0}, [hbm] + [anywhere] * 4,
         )
         return (new_g, new_u, new_d, *state)
 

time: 683 us -> 602 us (0.88)
  Pallas kernels: 589 us -> 512 us
    pallas_call x5 -> x6, Pallas kernels: 168 us -> 91.8 us  [call_local(): pl.pallas_call(body, out_shape=outs, in_specs=specs or [hbm] * len(ins),...]
    ppermute x20 -> x24, waiting for transfers between devices: 70.5 us -> 64.4 us  [permute(): return lax.ppermute(array, 'dp', pairs)]
  transfers between devices with their start and end apart: 20 -> 24, of which waited for: 6 -> 9; matrix products, arithmetic and copies ran while one was open for 0% -> 0% of each run, Pallas kernels for 15% -> 15%
where the time goes in v5:
time: 602 us
  Pallas kernels  512 us (85%)
  waiting for transfers between devices  64.4 us (11%)
  starting transfers between devices  13 us (2%)
  local copies, waits for them, and re-layouts  11 us (2%)
    pallas_call x1, Pallas kernels, step(): pl.pallas_call(kernel, out_shape=[*shapes(whole + block, BF16), jax.Shape...  420 us
    pallas_call x6, Pallas kernels, call_local(): pl.pallas_call(body, out_shape=outs, in_specs=specs or [hbm] * len(ins),...  91.8 us
    ppermute x24, waiting for transfers between devices, permute(): return lax.ppermute(array, 'dp', pairs)  64.4 us
    ppermute x24, starting transfers between devices, permute(): return lax.ppermute(array, 'dp', pairs)  13 us
  transfers between devices with their start and end apart: 24, of which 9 were waited for; matrix products, arithmetic and copies ran while one was open for 0% of the time, Pallas kernels for 15%

profile of v5, /device:TPU:0, one launch (start us, length us, event | category | flops | bytes accessed | tf_op | source)
XLA Modules:
  0.0 601.5 jit_solution(1609722993581326285)
XLA Ops:
  0.6 420.4 %step.1 = (bf16[2,1024,4096]{2,1,0:T(8,128)(2,1)}, bf16[2,1024,4096]{2,1,0:T(8,128)(2,1)}, bf16[2,4096,1024]{2,1,0:T(8,128)(2,1)}, bf16[2,64,4096]{2,1,0:T(8,128...) custom-call(bf16[1,2,1024,4096]{3,2,1,0:T(8,128)(2,1)} %refs_0_.1, ...), custom_call_target="tpu_custom_call" | custom-call | tf_op jit(solution)/shard_map/step/pallas_call | solution.py:443
  422.1 1.0 collective-permute-start.9
  424.2 1.0 collective-permute-start.3
  425.2 10.9 %collective-permute-done.8.refs_15_ = bf16[256,1024]{1,0:T(8,128)(2,1)S(1)} collective-permute-done((bf16[256,1024]{1,0:T(8,128)(2,1)}, bf16[256,1024]{1,0:T(8,128)(2,1)S(1)}, u32[]{:S(2)}, u32[]{:S(2)}) %collective-permute-start.8) | collective-permute-done | bytes 524320 | tf_op jit(solution)/shard_map/ppermute | solution.py:432
  438.0 1.3 collective-permute-start.17
  440.9 23.4 %collective-permute-done.16.refs_1_ = bf16[128,1024]{1,0:T(8,128)(2,1)S(1)} collective-permute-done((bf16[128,1024]{1,0:T(8,128)(2,1)S(1)}, bf16[128,1024]{1,0:T(8,128)(2,1)S(1)}, u32[]{:S(2)}, u32[]{:S(2)}) %collective-permute-start.16) | collective-permute-done | bytes 262176 | tf_op jit(solution)/shard_map/ppermute | solution.py:432
  464.8 3.5 collective-permute-done.20.refs_1_
  468.2 1.3 collective-permute-start.21
  470.3 1.3 collective-permute-start.13
  471.6 5.9 collective-permute-done.21.refs_2_
  480.8 12.0 %collective-permute-done.12.refs_2_ = bf16[2,64,4096]{2,1,0:T(8,128)(2,1)S(1)} collective-permute-done((bf16[2,64,4096]{2,1,0:T(8,128)(2,1)S(1)}, bf16[2,64,4096]{2,1,0:T(8,128)(2,1)S(1)}, u32[]{:S(2)}, u32[]{:S(2)}) %collective-permute-start.12) | collective-permute-done | bytes 1048608 | tf_op jit(solution)/shard_map/ppermute | solution.py:432
  492.8 4.6 collective-permute-done.13.refs_3_
  497.8 2.5 collective-permute-done.18.refs_3_
  501.7 1.2 copy-done.2
  503.0 1.2 copy-done.3
  504.2 1.2 copy-done.4
  506.1 17.5 %shard_map.188 = (bf16[2,4096,1024]{2,1,0:T(8,128)(2,1)}, f32[2,64,4096]{2,1,0:T(8,128)}, f32[2,64,4096]{2,1,0:T(8,128)}, f32[2,256,1024]{2,1,0:T(8,128)}, f32[2...) custom-call(f32[8,128]{1,0:T(8,128)S(1)} %copy-done.15, ...), custom_call_target="tpu_custom_call" | custom-call | flops 2013265920 | bytes 50331648 | tf_op jit(solution)/shard_map/pallas_call | solution.py:420
  523.6 14.9 %shard_map.187 = (bf16[2,1024,4096]{2,1,0:T(8,128)(2,1)}, bf16[2,1024,4096]{2,1,0:T(8,128)(2,1)}) custom-call(bf16[2,1024,4096]{2,1,0:T(8,128)(2,1)} %get-tuple-element.34.xg, bf16[2,1024,4096]{2,1,0:T(8,128)(2,1)} %get-tuple-element.35.xu), custom_call_target="tpu_custom_call" | custom-call | flops 1677721600 | bytes 41943040 | tf_op jit(solution)/shard_map/pallas_call | solution.py:420
  539.9 1.0 copy-done.10
  541.0 1.0 copy-done.12
  542.0 6.1 %shard_map.189 = (bf16[2,1024,4096]{2,1,0:T(8,128)(2,1)}, bf16[2,1024,4096]{2,1,0:T(8,128)(2,1)}, bf16[2,4096,1024]{2,1,0:T(8,128)(2,1)}) custom-call(bf16[2,1024,4096]{2,1,0:T(8,128)(2,1)} %get-tuple-element.36.refs_0_, bf16[2,1024,4096]{2,1,0:T(8,128)(2,1)} %get-tuple-element.37.refs_1_, ...), custom_call_target="tpu_custom_call", output_to_operand_aliasing={{0}: (0, {}), {1}: (1, {}), {2}: (2, {})} | custom-call | flops 1006632960 | bytes 25165824 | tf_op jit(solution)/shard_map/pallas_call | solution.py:420
  548.2 17.1 %shard_map.191.refs_0_ = bf16[2,4096,1024]{2,1,0:T(8,128)(2,1)} custom-call(bf16[2,4096,1024]{2,1,0:T(8,128)(2,1)} %get-tuple-element.52.refs_0_, bf16[128,1024]{1,0:T(8,128)(2,1)S(1)} %collective-permute-done.16.refs_1_, bf16[128,1024]{1,0:T(8,128)(2,1)} %collective-permute-done.17.refs_2_, ...), custom_call_target="tpu_custom_call", output_to_operand_aliasing={{}: (0, {})} | custom-call | flops 83886080 | bytes 2097152 | tf_op jit(solution)/shard_map/pallas_call | solution.py:420
  565.3 32.9 %shard_map.192 = bf16[2,4096,1024]{2,1,0:T(8,128)(2,1)} custom-call(bf16[2,4096,1024]{2,1,0:T(8,128)(2,1)} %shard_map.191.refs_0_, bf16[128,1024]{1,0:T(8,128)(2,1)} %collective-permute-done.20.refs_1_, bf16[128,1024]{1,0:T(8,128)(2,1)} %collective-permute-done.21.refs_2_, ...), custom_call_target="tpu_custom_call", output_to_operand_aliasing={{}: (0, {})} | custom-call | flops 83886080 | bytes 2097152 | tf_op jit(solution)/shard_map/pallas_call | solution.py:420
  598.3 3.3 shard_map.190
  (65 shorter events, 13.9 us)
Async XLA Ops:
  421.1 15.1 %collective-permute-start.8 = (bf16[256,1024]{1,0:T(8,128)(2,1)}, bf16[256,1024]{1,0:T(8,128)(2,1)S(1)}, u32[]{:S(2)}, u32[]{:S(2)}) collective-permute-start(bf16[256,1024]{1,0:T(8,128)(2,1)} %get-tuple-element.46.refs_11_), channel_id=1, source_target_pairs={{0,2},{1,3},{2,4},{3,5},{4,6},{5,7},{6,14},{7,15},{14,12},{15,13},... | collective-permute-start | bytes 1572872 | tf_op jit(solution)/shard_map/ppermute | solution.py:432
  422.1 15.0 %collective-permute-start.9 = (bf16[256,1024]{1,0:T(8,128)(2,1)}, bf16[256,1024]{1,0:T(8,128)(2,1)S(1)}, u32[]{:S(2)}, u32[]{:S(2)}) collective-permute-start(bf16[256,1024]{1,0:T(8,128)(2,1)} %get-tuple-element.47.refs_12_), channel_id=1, source_target_pairs={{2,0},{3,1},{4,2},{5,3},{6,4},{7,5},{14,6},{15,7},{12,14},{13,15},... | collective-permute-start | bytes 1572872 | tf_op jit(solution)/shard_map/ppermute | solution.py:432
  423.2 46.4 %collective-permute-start.2 = (bf16[2,64,4096]{2,1,0:T(8,128)(2,1)}, bf16[2,64,4096]{2,1,0:T(8,128)(2,1)S(1)}, u32[]{:S(2)}, u32[]{:S(2)}) collective-permute-start(bf16[2,64,4096]{2,1,0:T(8,128)(2,1)} %get-tuple-element.44.refs_3_), channel_id=1, source_target_pairs={{0,2},{1,3},{2,4},{3,5},{4,6},{5,7},{6,14},{7,15},{14,12},{15,13},... | collective-permute-start | bytes 3145736 | tf_op jit(solution)/shard_map/ppermute | solution.py:432
  424.2 46.1 %collective-permute-start.3 = (bf16[2,64,4096]{2,1,0:T(8,128)(2,1)}, bf16[2,64,4096]{2,1,0:T(8,128)(2,1)S(1)}, u32[]{:S(2)}, u32[]{:S(2)}) collective-permute-start(bf16[2,64,4096]{2,1,0:T(8,128)(2,1)} %get-tuple-element.45.refs_4_), channel_id=1, source_target_pairs={{2,0},{3,1},{4,2},{5,3},{6,4},{7,5},{14,6},{15,7},{12,14},{13,15},... | collective-permute-start | bytes 3145736 | tf_op jit(solution)/shard_map/ppermute | solution.py:432
  425.2 12.8 %collective-permute-start.6 = (bf16[256,1024]{1,0:T(8,128)(2,1)}, bf16[256,1024]{1,0:T(8,128)(2,1)S(1)}, u32[]{:S(2)}, u32[]{:S(2)}) collective-permute-start(bf16[256,1024]{1,0:T(8,128)(2,1)} %get-tuple-element.46.refs_11_), channel_id=1, source_target_pairs={{0,1},{1,0},{2,3},{3,2},{4,5},{5,4},{6,7},{7,6},{8,9},{9,8},{10,11... | collective-permute-start | bytes 1572872 | tf_op jit(solution)/shard_map/ppermute | solution.py:432
  436.2 3.1 collective-permute-start.7
  437.1 27.1 %collective-permute-start.16 = (bf16[128,1024]{1,0:T(8,128)(2,1)S(1)}, bf16[128,1024]{1,0:T(8,128)(2,1)S(1)}, u32[]{:S(2)}, u32[]{:S(2)}) collective-permute-start(bf16[128,1024]{1,0:T(8,128)(2,1)S(1)} %get-tuple-element.62), channel_id=1, source_target_pairs={{0,2},{1,3},{2,4},{3,5},{4,6},{5,7},{6,14},{7,15},{14,12},{15,13},... | collective-permute-start | bytes 786440 | tf_op jit(solution)/shard_map/ppermute | solution.py:432
  438.0 26.3 %collective-permute-start.17 = (bf16[128,1024]{1,0:T(8,128)(2,1)S(1)}, bf16[128,1024]{1,0:T(8,128)(2,1)}, u32[]{:S(2)}, u32[]{:S(2)}) collective-permute-start(bf16[128,1024]{1,0:T(8,128)(2,1)S(1)} %get-tuple-element.60), channel_id=1, source_target_pairs={{2,0},{3,1},{4,2},{5,3},{6,4},{7,5},{14,6},{15,7},{12,14},{13,15},... | collective-permute-start | bytes 786440 | tf_op jit(solution)/shard_map/ppermute | solution.py:432
  440.1 28.2 %collective-permute-start.20 = (bf16[128,1024]{1,0:T(8,128)(2,1)S(1)}, bf16[128,1024]{1,0:T(8,128)(2,1)}, u32[]{:S(2)}, u32[]{:S(2)}) collective-permute-start(bf16[128,1024]{1,0:T(8,128)(2,1)S(1)} %get-tuple-element.61), channel_id=1, source_target_pairs={{0,2},{1,3},{2,4},{3,5},{4,6},{5,7},{6,14},{7,15},{14,12},{15,13},... | collective-permute-start | bytes 786440 | tf_op jit(solution)/shard_map/ppermute | solution.py:432
  464.2 16.1 %collective-permute-start = (bf16[2,64,4096]{2,1,0:T(8,128)(2,1)}, bf16[2,64,4096]{2,1,0:T(8,128)(2,1)S(1)}, u32[]{:S(2)}, u32[]{:S(2)}) collective-permute-start(bf16[2,64,4096]{2,1,0:T(8,128)(2,1)} %get-tuple-element.44.refs_3_), channel_id=1, source_target_pairs={{0,1},{1,0},{2,3},{3,2},{4,5},{5,4},{6,7},{7,6},{8,9},{9,8},{10,11... | collective-permute-start | bytes 3145736 | tf_op jit(solution)/shard_map/ppermute | solution.py:432
  464.2 13.3 %collective-permute-start.10 = (bf16[256,1024]{1,0:T(8,128)(2,1)S(1)}, bf16[256,1024]{1,0:T(8,128)(2,1)S(1)}, u32[]{:S(2)}, u32[]{:S(2)}) collective-permute-start(bf16[256,1024]{1,0:T(8,128)(2,1)S(1)} %collective-permute-done.8.refs_15_), channel_id=1, source_target_pairs={{0,1},{1,0},{2,3},{3,2},{4,5},{5,4},{6,7},{7,6},{8,9},{9,8},{10,11... | collective-permute-start | bytes 1572872 | tf_op jit(solution)/shard_map/ppermute | solution.py:432
  468.2 9.3 %collective-permute-start.21 = (bf16[128,1024]{1,0:T(8,128)(2,1)S(1)}, bf16[128,1024]{1,0:T(8,128)(2,1)}, u32[]{:S(2)}, u32[]{:S(2)}) collective-permute-start(bf16[128,1024]{1,0:T(8,128)(2,1)S(1)} %get-tuple-element.59), channel_id=1, source_target_pairs={{2,0},{3,1},{4,2},{5,3},{6,4},{7,5},{14,6},{15,7},{12,14},{13,15},... | collective-permute-start | bytes 786440 | tf_op jit(solution)/shard_map/ppermute | solution.py:432
  469.6 23.2 %collective-permute-start.12 = (bf16[2,64,4096]{2,1,0:T(8,128)(2,1)S(1)}, bf16[2,64,4096]{2,1,0:T(8,128)(2,1)S(1)}, u32[]{:S(2)}, u32[]{:S(2)}) collective-permute-start(bf16[2,64,4096]{2,1,0:T(8,128)(2,1)S(1)} %collective-permute-done.2.refs_7_), channel_id=1, source_target_pairs={{0,2},{1,3},{2,4},{3,5},{4,6},{5,7},{6,14},{7,15},{14,12},{15,13},... | collective-permute-start | bytes 3145736 | tf_op jit(solution)/shard_map/ppermute | solution.py:432
  470.3 27.0 %collective-permute-start.13 = (bf16[2,64,4096]{2,1,0:T(8,128)(2,1)S(1)}, bf16[2,64,4096]{2,1,0:T(8,128)(2,1)S(1)}, u32[]{:S(2)}, u32[]{:S(2)}) collective-permute-start(bf16[2,64,4096]{2,1,0:T(8,128)(2,1)S(1)} %collective-permute-done.3.refs_8_), channel_id=1, source_target_pairs={{2,0},{3,1},{4,2},{5,3},{6,4},{7,5},{14,6},{15,7},{12,14},{13,15},... | collective-permute-start | bytes 3145736 | tf_op jit(solution)/shard_map/ppermute | solution.py:432
  477.5 1.9 collective-permute-start.11
  478.3 19.0 %collective-permute-start.1 = (bf16[2,64,4096]{2,1,0:T(8,128)(2,1)}, bf16[2,64,4096]{2,1,0:T(8,128)(2,1)S(1)}, u32[]{:S(2)}, u32[]{:S(2)}) collective-permute-start(bf16[2,64,4096]{2,1,0:T(8,128)(2,1)} %get-tuple-element.45.refs_4_), channel_id=1, source_target_pairs={{0,1},{1,0},{2,3},{3,2},{4,5},{5,4},{6,7},{7,6},{8,9},{9,8},{10,11... | collective-permute-start | bytes 3145736 | tf_op jit(solution)/shard_map/ppermute | solution.py:432
  480.2 21.0 %collective-permute-start.4 = (bf16[2,64,4096]{2,1,0:T(8,128)(2,1)S(1)}, bf16[2,64,4096]{2,1,0:T(8,128)(2,1)S(1)}, u32[]{:S(2)}, u32[]{:S(2)}) collective-permute-start(bf16[2,64,4096]{2,1,0:T(8,128)(2,1)S(1)} %collective-permute-done.2.refs_7_), channel_id=1, source_target_pairs={{0,1},{1,0},{2,3},{3,2},{4,5},{5,4},{6,7},{7,6},{8,9},{9,8},{10,11... | collective-permute-start | bytes 3145736 | tf_op jit(solution)/shard_map/ppermute | solution.py:432
  480.4 21.2 %collective-permute-start.5 = (bf16[2,64,4096]{2,1,0:T(8,128)(2,1)S(1)}, bf16[2,64,4096]{2,1,0:T(8,128)(2,1)S(1)}, u32[]{:S(2)}, u32[]{:S(2)}) collective-permute-start(bf16[2,64,4096]{2,1,0:T(8,128)(2,1)S(1)} %collective-permute-done.3.refs_8_), channel_id=1, source_target_pairs={{0,1},{1,0},{2,3},{3,2},{4,5},{5,4},{6,7},{7,6},{8,9},{9,8},{10,11... | collective-permute-start | bytes 3145736 | tf_op jit(solution)/shard_map/ppermute | solution.py:432
  492.8 105.5 %collective-permute-start.14 = (bf16[2,64,4096]{2,1,0:T(8,128)(2,1)S(1)}, bf16[2,64,4096]{2,1,0:T(8,128)(2,1)S(1)}, u32[]{:S(2)}, u32[]{:S(2)}) collective-permute-start(bf16[2,64,4096]{2,1,0:T(8,128)(2,1)S(1)} %collective-permute-done.12.refs_2_), channel_id=1, source_target_pairs={{0,1},{1,0},{2,3},{3,2},{4,5},{5,4},{6,7},{7,6},{8,9},{9,8},{10,11... | collective-permute-start | bytes 3145736 | tf_op jit(solution)/shard_map/ppermute | solution.py:432
  497.3 100.9 %collective-permute-start.15 = (bf16[2,64,4096]{2,1,0:T(8,128)(2,1)S(1)}, bf16[2,64,4096]{2,1,0:T(8,128)(2,1)}, u32[]{:S(2)}, u32[]{:S(2)}) collective-permute-start(bf16[2,64,4096]{2,1,0:T(8,128)(2,1)S(1)} %collective-permute-done.13.refs_3_), channel_id=1, source_target_pairs={{0,1},{1,0},{2,3},{3,2},{4,5},{5,4},{6,7},{7,6},{8,9},{9,8},{10,11... | collective-permute-start | bytes 3145736 | tf_op jit(solution)/shard_map/ppermute | solution.py:432
  497.3 3.0 collective-permute-start.18
  501.1 47.1 %collective-permute-start.19 = (bf16[128,1024]{1,0:T(8,128)(2,1)}, bf16[128,1024]{1,0:T(8,128)(2,1)}, u32[]{:S(2)}, u32[]{:S(2)}) collective-permute-start(bf16[128,1024]{1,0:T(8,128)(2,1)} %collective-permute-done.17.refs_2_), channel_id=1, source_target_pairs={{0,1},{1,0},{2,3},{3,2},{4,5},{5,4},{6,7},{7,6},{8,9},{9,8},{10,11... | collective-permute-start | bytes 786440 | tf_op jit(solution)/shard_map/ppermute | solution.py:432
  501.2 64.1 %collective-permute-start.22 = (bf16[128,1024]{1,0:T(8,128)(2,1)}, bf16[128,1024]{1,0:T(8,128)(2,1)}, u32[]{:S(2)}, u32[]{:S(2)}) collective-permute-start(bf16[128,1024]{1,0:T(8,128)(2,1)} %collective-permute-done.20.refs_1_), channel_id=1, source_target_pairs={{0,1},{1,0},{2,3},{3,2},{4,5},{5,4},{6,7},{7,6},{8,9},{9,8},{10,11... | collective-permute-start | bytes 786440 | tf_op jit(solution)/shard_map/ppermute | solution.py:432
  501.6 63.7 %collective-permute-start.23 = (bf16[128,1024]{1,0:T(8,128)(2,1)}, bf16[128,1024]{1,0:T(8,128)(2,1)}, u32[]{:S(2)}, u32[]{:S(2)}) collective-permute-start(bf16[128,1024]{1,0:T(8,128)(2,1)} %collective-permute-done.21.refs_2_), channel_id=1, source_target_pairs={{0,1},{1,0},{2,3},{3,2},{4,5},{5,4},{6,7},{7,6},{8,9},{9,8},{10,11... | collective-permute-start | bytes 786440 | tf_op jit(solution)/shard_map/ppermute | solution.py:432
  (16 other events, 76.8 us)

commit v6 on v5

--- a/solution.py
+++ b/solution.py
@@ -393,8 +393,12 @@
     in_place(landed(LAST + 2, refs[1:5], refs[5:6], 0, pl.ds(0, 128)), refs[6])
 
 
+def finish_own(*refs):
+    in_place(landed(LAST + 2, refs[1:3], refs[3:4], 0, pl.ds(128, 128)), refs[4])
+
+
 def finish_tail(*refs):
-    in_place(landed(LAST + 2, refs[1:5], refs[5:6], 0, pl.ds(128, 128)), refs[6])
+    in_place(landed(LAST + 2, refs[1:3], refs[3:4], 2, pl.ds(128, 128)), refs[4])
 
 
 def solution(mesh):
@@ -516,10 +520,10 @@
             finish_deep, shapes(whole[2:], BF16), (news[2], *deep7, *their_deep7), [dma((4,))],
             2 * mib, 24, {0: 0}, [hbm] + [anywhere] * 4,
         )
-        (new_d,) = local(
-            finish_tail, shapes(whole[2:], BF16), (new_d, *tail7, *their_tail7), [dma((4,))], 2 * mib, 24,
-            {0: 0}, [hbm] + [anywhere] * 4,
-        )
+        for body, lands in ((finish_own, tail7), (finish_tail, their_tail7)):
+            (new_d,) = local(
+                body, shapes(whole[2:], BF16), (new_d, *lands), [dma((2,))], mib, 24, {0: 0}, [hbm] + [anywhere] * 2
+            )
         return (new_g, new_u, new_d, *state)
 
     all_of, cut = P(None, None, None), P(None, "dp", None)

time: 602 us -> 603 us (level)
    pallas_call x6 -> x7, Pallas kernels: 91.8 us -> 93 us  [call_local(): pl.pallas_call(body, out_shape=outs, in_specs=specs or [hbm] * len(ins),...]
where the time goes in v6:
time: 603 us
  Pallas kernels  513 us (85%)
  waiting for transfers between devices  64.4 us (11%)
  starting transfers between devices  13.1 us (2%)
  local copies, waits for them, and re-layouts  11 us (2%)
    pallas_call x1, Pallas kernels, step(): pl.pallas_call(kernel, out_shape=[*shapes(whole + block, BF16), jax.Shape...  420 us
    pallas_call x7, Pallas kernels, call_local(): pl.pallas_call(body, out_shape=outs, in_specs=specs or [hbm] * len(ins),...  93 us
    ppermute x24, waiting for transfers between devices, permute(): return lax.ppermute(array, 'dp', pairs)  64.4 us
    ppermute x24, starting transfers between devices, permute(): return lax.ppermute(array, 'dp', pairs)  13.1 us
  transfers between devices with their start and end apart: 24, of which 9 were waited for; matrix products, arithmetic and copies ran while one was open for 0% of the time, Pallas kernels for 15%

profile of v6, /device:TPU:0, one launch (start us, length us, event | category | flops | bytes accessed | tf_op | source)
XLA Modules:
  0.0 602.7 jit_solution(14038095115635993047)
XLA Ops:
  0.6 420.4 %step.1 = (bf16[2,1024,4096]{2,1,0:T(8,128)(2,1)}, bf16[2,1024,4096]{2,1,0:T(8,128)(2,1)}, bf16[2,4096,1024]{2,1,0:T(8,128)(2,1)}, bf16[2,64,4096]{2,1,0:T(8,128...) custom-call(bf16[1,2,1024,4096]{3,2,1,0:T(8,128)(2,1)} %refs_0_.1, ...), custom_call_target="tpu_custom_call" | custom-call | tf_op jit(solution)/shard_map/step/pallas_call | solution.py:447
  422.1 1.0 collective-permute-start.9
  424.2 1.0 collective-permute-start.3
  425.2 10.9 %collective-permute-done.8.refs_15_ = bf16[256,1024]{1,0:T(8,128)(2,1)S(1)} collective-permute-done((bf16[256,1024]{1,0:T(8,128)(2,1)}, bf16[256,1024]{1,0:T(8,128)(2,1)S(1)}, u32[]{:S(2)}, u32[]{:S(2)}) %collective-permute-start.8) | collective-permute-done | bytes 524320 | tf_op jit(solution)/shard_map/ppermute | solution.py:436
  438.0 1.3 collective-permute-start.17
  440.9 23.4 %collective-permute-done.16.refs_1_ = bf16[128,1024]{1,0:T(8,128)(2,1)S(1)} collective-permute-done((bf16[128,1024]{1,0:T(8,128)(2,1)S(1)}, bf16[128,1024]{1,0:T(8,128)(2,1)S(1)}, u32[]{:S(2)}, u32[]{:S(2)}) %collective-permute-start.16) | collective-permute-done | bytes 262176 | tf_op jit(solution)/shard_map/ppermute | solution.py:436
  464.7 3.5 collective-permute-done.20.refs_1_
  468.2 1.3 collective-permute-start.21
  470.3 1.3 collective-permute-start.13
  471.6 5.9 collective-permute-done.21.refs_2_
  480.8 12.0 %collective-permute-done.12.refs_2_ = bf16[2,64,4096]{2,1,0:T(8,128)(2,1)S(1)} collective-permute-done((bf16[2,64,4096]{2,1,0:T(8,128)(2,1)S(1)}, bf16[2,64,4096]{2,1,0:T(8,128)(2,1)S(1)}, u32[]{:S(2)}, u32[]{:S(2)}) %collective-permute-start.12) | collective-permute-done | bytes 1048608 | tf_op jit(solution)/shard_map/ppermute | solution.py:436
  492.7 4.6 collective-permute-done.13.refs_3_
  497.8 2.5 collective-permute-done.18.refs_3_
  501.2 1.2 copy-done.2
  502.4 1.2 copy-done.3
  503.6 1.2 copy-done.4
  505.5 17.5 %shard_map.188 = (bf16[2,4096,1024]{2,1,0:T(8,128)(2,1)}, f32[2,64,4096]{2,1,0:T(8,128)}, f32[2,64,4096]{2,1,0:T(8,128)}, f32[2,256,1024]{2,1,0:T(8,128)}, f32[2...) custom-call(f32[8,128]{1,0:T(8,128)S(1)} %copy-done.15, ...), custom_call_target="tpu_custom_call" | custom-call | flops 2013265920 | bytes 50331648 | tf_op jit(solution)/shard_map/pallas_call | solution.py:424
  523.7 14.9 %shard_map.187 = (bf16[2,1024,4096]{2,1,0:T(8,128)(2,1)}, bf16[2,1024,4096]{2,1,0:T(8,128)(2,1)}) custom-call(bf16[2,1024,4096]{2,1,0:T(8,128)(2,1)} %get-tuple-element.34.xg, bf16[2,1024,4096]{2,1,0:T(8,128)(2,1)} %get-tuple-element.35.xu), custom_call_target="tpu_custom_call" | custom-call | flops 1677721600 | bytes 41943040 | tf_op jit(solution)/shard_map/pallas_call | solution.py:424
  539.0 1.0 copy-done.8
  542.1 6.1 %shard_map.189 = (bf16[2,1024,4096]{2,1,0:T(8,128)(2,1)}, bf16[2,1024,4096]{2,1,0:T(8,128)(2,1)}, bf16[2,4096,1024]{2,1,0:T(8,128)(2,1)}) custom-call(bf16[2,1024,4096]{2,1,0:T(8,128)(2,1)} %get-tuple-element.36.refs_0_, bf16[2,1024,4096]{2,1,0:T(8,128)(2,1)} %get-tuple-element.37.refs_1_, ...), custom_call_target="tpu_custom_call", output_to_operand_aliasing={{0}: (0, {}), {1}: (1, {}), {2}: (2, {})} | custom-call | flops 1006632960 | bytes 25165824 | tf_op jit(solution)/shard_map/pallas_call | solution.py:424
  548.2 17.1 %shard_map.191.refs_0_ = bf16[2,4096,1024]{2,1,0:T(8,128)(2,1)} custom-call(bf16[2,4096,1024]{2,1,0:T(8,128)(2,1)} %get-tuple-element.52.refs_0_, bf16[128,1024]{1,0:T(8,128)(2,1)S(1)} %collective-permute-done.16.refs_1_, bf16[128,1024]{1,0:T(8,128)(2,1)} %collective-permute-done.17.refs_2_, ...), custom_call_target="tpu_custom_call", output_to_operand_aliasing={{}: (0, {})} | custom-call | flops 83886080 | bytes 2097152 | tf_op jit(solution)/shard_map/pallas_call | solution.py:424
  565.3 17.0 %shard_map.192.refs_0_ = bf16[2,4096,1024]{2,1,0:T(8,128)(2,1)} custom-call(bf16[2,4096,1024]{2,1,0:T(8,128)(2,1)} %shard_map.191.refs_0_, bf16[128,1024]{1,0:T(8,128)(2,1)} %collective-permute-done.20.refs_1_, bf16[128,1024]{1,0:T(8,128)(2,1)} %collective-permute-done.21.refs_2_), custom_call_target="tpu_custom_call", output_to_operand_aliasing={{}: (0, {})} | custom-call | flops 41943040 | bytes 1048576 | tf_op jit(solution)/shard_map/pallas_call | solution.py:424
  582.4 17.0 %shard_map.193 = bf16[2,4096,1024]{2,1,0:T(8,128)(2,1)} custom-call(bf16[2,4096,1024]{2,1,0:T(8,128)(2,1)} %shard_map.192.refs_0_, bf16[128,1024]{1,0:T(8,128)(2,1)} %collective-permute-done.22.refs_1_, bf16[128,1024]{1,0:T(8,128)(2,1)} %collective-permute-done.23.refs_2_), custom_call_target="tpu_custom_call", output_to_operand_aliasing={{}: (0, {})} | custom-call | flops 41943040 | bytes 1048576 | tf_op jit(solution)/shard_map/pallas_call | solution.py:424
  599.5 3.3 shard_map.190
  (66 shorter events, 15.0 us)
Async XLA Ops:
  421.1 15.1 %collective-permute-start.8 = (bf16[256,1024]{1,0:T(8,128)(2,1)}, bf16[256,1024]{1,0:T(8,128)(2,1)S(1)}, u32[]{:S(2)}, u32[]{:S(2)}) collective-permute-start(bf16[256,1024]{1,0:T(8,128)(2,1)} %get-tuple-element.46.refs_11_), channel_id=1, source_target_pairs={{0,2},{1,3},{2,4},{3,5},{4,6},{5,7},{6,14},{7,15},{14,12},{15,13},... | collective-permute-start | bytes 1572872 | tf_op jit(solution)/shard_map/ppermute | solution.py:436
  422.1 15.0 %collective-permute-start.9 = (bf16[256,1024]{1,0:T(8,128)(2,1)}, bf16[256,1024]{1,0:T(8,128)(2,1)S(1)}, u32[]{:S(2)}, u32[]{:S(2)}) collective-permute-start(bf16[256,1024]{1,0:T(8,128)(2,1)} %get-tuple-element.47.refs_12_), channel_id=1, source_target_pairs={{2,0},{3,1},{4,2},{5,3},{6,4},{7,5},{14,6},{15,7},{12,14},{13,15},... | collective-permute-start | bytes 1572872 | tf_op jit(solution)/shard_map/ppermute | solution.py:436
  423.2 46.4 %collective-permute-start.2 = (bf16[2,64,4096]{2,1,0:T(8,128)(2,1)}, bf16[2,64,4096]{2,1,0:T(8,128)(2,1)S(1)}, u32[]{:S(2)}, u32[]{:S(2)}) collective-permute-start(bf16[2,64,4096]{2,1,0:T(8,128)(2,1)} %get-tuple-element.44.refs_3_), channel_id=1, source_target_pairs={{0,2},{1,3},{2,4},{3,5},{4,6},{5,7},{6,14},{7,15},{14,12},{15,13},... | collective-permute-start | bytes 3145736 | tf_op jit(solution)/shard_map/ppermute | solution.py:436
  424.2 46.1 %collective-permute-start.3 = (bf16[2,64,4096]{2,1,0:T(8,128)(2,1)}, bf16[2,64,4096]{2,1,0:T(8,128)(2,1)S(1)}, u32[]{:S(2)}, u32[]{:S(2)}) collective-permute-start(bf16[2,64,4096]{2,1,0:T(8,128)(2,1)} %get-tuple-element.45.refs_4_), channel_id=1, source_target_pairs={{2,0},{3,1},{4,2},{5,3},{6,4},{7,5},{14,6},{15,7},{12,14},{13,15},... | collective-permute-start | bytes 3145736 | tf_op jit(solution)/shard_map/ppermute | solution.py:436
  425.2 12.8 %collective-permute-start.6 = (bf16[256,1024]{1,0:T(8,128)(2,1)}, bf16[256,1024]{1,0:T(8,128)(2,1)S(1)}, u32[]{:S(2)}, u32[]{:S(2)}) collective-permute-start(bf16[256,1024]{1,0:T(8,128)(2,1)} %get-tuple-element.46.refs_11_), channel_id=1, source_target_pairs={{0,1},{1,0},{2,3},{3,2},{4,5},{5,4},{6,7},{7,6},{8,9},{9,8},{10,11... | collective-permute-start | bytes 1572872 | tf_op jit(solution)/shard_map/ppermute | solution.py:436
  436.1 3.1 collective-permute-start.7
  437.1 27.1 %collective-permute-start.16 = (bf16[128,1024]{1,0:T(8,128)(2,1)S(1)}, bf16[128,1024]{1,0:T(8,128)(2,1)S(1)}, u32[]{:S(2)}, u32[]{:S(2)}) collective-permute-start(bf16[128,1024]{1,0:T(8,128)(2,1)S(1)} %get-tuple-element.62), channel_id=1, source_target_pairs={{0,2},{1,3},{2,4},{3,5},{4,6},{5,7},{6,14},{7,15},{14,12},{15,13},... | collective-permute-start | bytes 786440 | tf_op jit(solution)/shard_map/ppermute | solution.py:436
  438.0 26.3 %collective-permute-start.17 = (bf16[128,1024]{1,0:T(8,128)(2,1)S(1)}, bf16[128,1024]{1,0:T(8,128)(2,1)}, u32[]{:S(2)}, u32[]{:S(2)}) collective-permute-start(bf16[128,1024]{1,0:T(8,128)(2,1)S(1)} %get-tuple-element.60), channel_id=1, source_target_pairs={{2,0},{3,1},{4,2},{5,3},{6,4},{7,5},{14,6},{15,7},{12,14},{13,15},... | collective-permute-start | bytes 786440 | tf_op jit(solution)/shard_map/ppermute | solution.py:436
  440.1 28.2 %collective-permute-start.20 = (bf16[128,1024]{1,0:T(8,128)(2,1)S(1)}, bf16[128,1024]{1,0:T(8,128)(2,1)}, u32[]{:S(2)}, u32[]{:S(2)}) collective-permute-start(bf16[128,1024]{1,0:T(8,128)(2,1)S(1)} %get-tuple-element.61), channel_id=1, source_target_pairs={{0,2},{1,3},{2,4},{3,5},{4,6},{5,7},{6,14},{7,15},{14,12},{15,13},... | collective-permute-start | bytes 786440 | tf_op jit(solution)/shard_map/ppermute | solution.py:436
  464.2 16.1 %collective-permute-start = (bf16[2,64,4096]{2,1,0:T(8,128)(2,1)}, bf16[2,64,4096]{2,1,0:T(8,128)(2,1)S(1)}, u32[]{:S(2)}, u32[]{:S(2)}) collective-permute-start(bf16[2,64,4096]{2,1,0:T(8,128)(2,1)} %get-tuple-element.44.refs_3_), channel_id=1, source_target_pairs={{0,1},{1,0},{2,3},{3,2},{4,5},{5,4},{6,7},{7,6},{8,9},{9,8},{10,11... | collective-permute-start | bytes 3145736 | tf_op jit(solution)/shard_map/ppermute | solution.py:436
  464.2 13.3 %collective-permute-start.10 = (bf16[256,1024]{1,0:T(8,128)(2,1)S(1)}, bf16[256,1024]{1,0:T(8,128)(2,1)S(1)}, u32[]{:S(2)}, u32[]{:S(2)}) collective-permute-start(bf16[256,1024]{1,0:T(8,128)(2,1)S(1)} %collective-permute-done.8.refs_15_), channel_id=1, source_target_pairs={{0,1},{1,0},{2,3},{3,2},{4,5},{5,4},{6,7},{7,6},{8,9},{9,8},{10,11... | collective-permute-start | bytes 1572872 | tf_op jit(solution)/shard_map/ppermute | solution.py:436
  468.2 9.3 %collective-permute-start.21 = (bf16[128,1024]{1,0:T(8,128)(2,1)S(1)}, bf16[128,1024]{1,0:T(8,128)(2,1)}, u32[]{:S(2)}, u32[]{:S(2)}) collective-permute-start(bf16[128,1024]{1,0:T(8,128)(2,1)S(1)} %get-tuple-element.59), channel_id=1, source_target_pairs={{2,0},{3,1},{4,2},{5,3},{6,4},{7,5},{14,6},{15,7},{12,14},{13,15},... | collective-permute-start | bytes 786440 | tf_op jit(solution)/shard_map/ppermute | solution.py:436
  469.6 23.2 %collective-permute-start.12 = (bf16[2,64,4096]{2,1,0:T(8,128)(2,1)S(1)}, bf16[2,64,4096]{2,1,0:T(8,128)(2,1)S(1)}, u32[]{:S(2)}, u32[]{:S(2)}) collective-permute-start(bf16[2,64,4096]{2,1,0:T(8,128)(2,1)S(1)} %collective-permute-done.2.refs_7_), channel_id=1, source_target_pairs={{0,2},{1,3},{2,4},{3,5},{4,6},{5,7},{6,14},{7,15},{14,12},{15,13},... | collective-permute-start | bytes 3145736 | tf_op jit(solution)/shard_map/ppermute | solution.py:436
  470.3 27.0 %collective-permute-start.13 = (bf16[2,64,4096]{2,1,0:T(8,128)(2,1)S(1)}, bf16[2,64,4096]{2,1,0:T(8,128)(2,1)S(1)}, u32[]{:S(2)}, u32[]{:S(2)}) collective-permute-start(bf16[2,64,4096]{2,1,0:T(8,128)(2,1)S(1)} %collective-permute-done.3.refs_8_), channel_id=1, source_target_pairs={{2,0},{3,1},{4,2},{5,3},{6,4},{7,5},{14,6},{15,7},{12,14},{13,15},... | collective-permute-start | bytes 3145736 | tf_op jit(solution)/shard_map/ppermute | solution.py:436
  477.5 1.9 collective-permute-start.11
  478.3 19.0 %collective-permute-start.1 = (bf16[2,64,4096]{2,1,0:T(8,128)(2,1)}, bf16[2,64,4096]{2,1,0:T(8,128)(2,1)S(1)}, u32[]{:S(2)}, u32[]{:S(2)}) collective-permute-start(bf16[2,64,4096]{2,1,0:T(8,128)(2,1)} %get-tuple-element.45.refs_4_), channel_id=1, source_target_pairs={{0,1},{1,0},{2,3},{3,2},{4,5},{5,4},{6,7},{7,6},{8,9},{9,8},{10,11... | collective-permute-start | bytes 3145736 | tf_op jit(solution)/shard_map/ppermute | solution.py:436
  480.2 42.8 %collective-permute-start.4 = (bf16[2,64,4096]{2,1,0:T(8,128)(2,1)S(1)}, bf16[2,64,4096]{2,1,0:T(8,128)(2,1)S(1)}, u32[]{:S(2)}, u32[]{:S(2)}) collective-permute-start(bf16[2,64,4096]{2,1,0:T(8,128)(2,1)S(1)} %collective-permute-done.2.refs_7_), channel_id=1, source_target_pairs={{0,1},{1,0},{2,3},{3,2},{4,5},{5,4},{6,7},{7,6},{8,9},{9,8},{10,11... | collective-permute-start | bytes 3145736 | tf_op jit(solution)/shard_map/ppermute | solution.py:436
  480.4 43.2 %collective-permute-start.5 = (bf16[2,64,4096]{2,1,0:T(8,128)(2,1)S(1)}, bf16[2,64,4096]{2,1,0:T(8,128)(2,1)S(1)}, u32[]{:S(2)}, u32[]{:S(2)}) collective-permute-start(bf16[2,64,4096]{2,1,0:T(8,128)(2,1)S(1)} %collective-permute-done.3.refs_8_), channel_id=1, source_target_pairs={{0,1},{1,0},{2,3},{3,2},{4,5},{5,4},{6,7},{7,6},{8,9},{9,8},{10,11... | collective-permute-start | bytes 3145736 | tf_op jit(solution)/shard_map/ppermute | solution.py:436
  492.7 106.7 %collective-permute-start.14 = (bf16[2,64,4096]{2,1,0:T(8,128)(2,1)S(1)}, bf16[2,64,4096]{2,1,0:T(8,128)(2,1)S(1)}, u32[]{:S(2)}, u32[]{:S(2)}) collective-permute-start(bf16[2,64,4096]{2,1,0:T(8,128)(2,1)S(1)} %collective-permute-done.12.refs_2_), channel_id=1, source_target_pairs={{0,1},{1,0},{2,3},{3,2},{4,5},{5,4},{6,7},{7,6},{8,9},{9,8},{10,11... | collective-permute-start | bytes 3145736 | tf_op jit(solution)/shard_map/ppermute | solution.py:436
  497.3 102.1 %collective-permute-start.15 = (bf16[2,64,4096]{2,1,0:T(8,128)(2,1)S(1)}, bf16[2,64,4096]{2,1,0:T(8,128)(2,1)}, u32[]{:S(2)}, u32[]{:S(2)}) collective-permute-start(bf16[2,64,4096]{2,1,0:T(8,128)(2,1)S(1)} %collective-permute-done.13.refs_3_), channel_id=1, source_target_pairs={{0,1},{1,0},{2,3},{3,2},{4,5},{5,4},{6,7},{7,6},{8,9},{9,8},{10,11... | collective-permute-start | bytes 3145736 | tf_op jit(solution)/shard_map/ppermute | solution.py:436
  497.3 3.0 collective-permute-start.18
  501.1 47.2 %collective-permute-start.19 = (bf16[128,1024]{1,0:T(8,128)(2,1)}, bf16[128,1024]{1,0:T(8,128)(2,1)}, u32[]{:S(2)}, u32[]{:S(2)}) collective-permute-start(bf16[128,1024]{1,0:T(8,128)(2,1)} %collective-permute-done.17.refs_2_), channel_id=1, source_target_pairs={{0,1},{1,0},{2,3},{3,2},{4,5},{5,4},{6,7},{7,6},{8,9},{9,8},{10,11... | collective-permute-start | bytes 786440 | tf_op jit(solution)/shard_map/ppermute | solution.py:436
  523.1 59.3 %collective-permute-start.22 = (bf16[128,1024]{1,0:T(8,128)(2,1)}, bf16[128,1024]{1,0:T(8,128)(2,1)}, u32[]{:S(2)}, u32[]{:S(2)}) collective-permute-start(bf16[128,1024]{1,0:T(8,128)(2,1)} %collective-permute-done.20.refs_1_), channel_id=1, source_target_pairs={{0,1},{1,0},{2,3},{3,2},{4,5},{5,4},{6,7},{7,6},{8,9},{9,8},{10,11... | collective-permute-start | bytes 786440 | tf_op jit(solution)/shard_map/ppermute | solution.py:436
  523.5 58.9 %collective-permute-start.23 = (bf16[128,1024]{1,0:T(8,128)(2,1)}, bf16[128,1024]{1,0:T(8,128)(2,1)}, u32[]{:S(2)}, u32[]{:S(2)}) collective-permute-start(bf16[128,1024]{1,0:T(8,128)(2,1)} %collective-permute-done.21.refs_2_), channel_id=1, source_target_pairs={{0,1},{1,0},{2,3},{3,2},{4,5},{5,4},{6,7},{7,6},{8,9},{9,8},{10,11... | collective-permute-start | bytes 786440 | tf_op jit(solution)/shard_map/ppermute | solution.py:436
  (16 other events, 76.8 us)
